TPU v7x, 512 devices: a whole 4x8x8 slice. The times are simulated.
512 devices in a mesh: freq: 32 (over x, z), sens: 16 (over y, core).
Axes of the slice: x: 4, y: 8, z: 8, core: 2. Of those that a mesh axis runs over, the one named last changes fastest.
Arguments:
- samples: bfloat16 [512, 640, 420], P('freq', 'sens'), may hold values from -6 to 6
- response_tiles: bfloat16 [448, 2, 640, 21], P('freq', None, 'sens'), may hold values from -0.25 to 0.25
- slot_sensor: int32 [640], P('sens'), may hold values from -1 to 599, as said below
- sensor_noise: float32 [600], replicated, may hold values from 0.02 to 5
- advance_offset: int32 [21], replicated, may hold values from 0 to 419
Outputs:
- outlook_values: bfloat16 [512, 21, 420], P('freq')
- noise_spread: float32 [21], replicated
Inputs may be any that keep to these rules, and one draw needn't show every extreme that they name: `slot_sensor`: every sensor number appears in exactly one slot; the other 40 slots hold -1.
All inputs are finite; a program needn't handle non-finite values.
Results may differ from a plain program's by a relative error of at most 0.0055.
Values may be sent and summed in bfloat16 or wider, within the bound.
No kernel may reach another device: no remote copies, remote signals or barrier semaphores. Data moves between devices by JAX's collectives and lax.ppermute only.
A program may use at most 64 MiB of HBM per device.

v0:
```python
import functools
import math

import jax
import jax.numpy as jnp
from jax import lax
from jax.sharding import Mesh
from jax.sharding import PartitionSpec as P

KEPT_HARMONICS = 448
FREQ = ("freq_0", "freq_1")
FREQ_SENS = ("freq_0", "freq_1", "sens_0", "sens_1")
SENS = ("sens_0", "sens_1")


def one_axis_at_a_time(array, axes):
    return functools.reduce(lax.psum, axes, array)


def copy_for_each(array, axis):
    devices = lax.axis_size(axis)
    return lax.all_to_all(
        jnp.broadcast_to(array[None], (devices, *array.shape)), axis, 0, 0, tiled=True
    )


def in_order(blocks, dim):
    shape = list(blocks.shape[1:])
    shape[dim] *= blocks.shape[0]
    return jnp.moveaxis(blocks, 0, dim).reshape(shape)


def collect(array, axis, dim):
    blocks = copy_for_each(array, axis)
    return in_order(blocks, dim)


def total_of_pieces(array, axis):
    blocks = lax.all_gather(array, axis)
    return blocks.sum(axis=0)


def angles(first_bin, bin_count, period, factor):
    bin_index = first_bin + lax.iota(jnp.int32, bin_count)
    turn_count = bin_index[:, None] * factor[None, :] % period
    return turn_count.astype(jnp.float32) * (2.0 * math.pi / period)


def forward_table(bin_count, step_count, period):
    phase_angle = angles(0, bin_count, period, lax.iota(jnp.int32, step_count))
    return jnp.stack([jnp.cos(phase_angle), -jnp.sin(phase_angle)]).astype(jnp.bfloat16)


def inverse_table(bin_count, step_count, period):
    bin_index = lax.iota(jnp.int32, bin_count)
    weight = jnp.where(bin_index == 0, 1.0, 2.0).astype(jnp.float32) / period
    phase_angle = angles(0, bin_count, period, lax.iota(jnp.int32, step_count))
    return jnp.stack(
        [weight[:, None] * jnp.cos(phase_angle), -weight[:, None] * jnp.sin(phase_angle)]
    )


def contract(spectra, blocks):

    def product(left, right):
        return jnp.einsum("krs,ksq->kqr", left, right, preferred_element_type=jnp.float32)

    real_part = product(spectra[0], blocks[:, 0]) - product(spectra[1], blocks[:, 1])
    imag_part = product(spectra[0], blocks[:, 1]) + product(spectra[1], blocks[:, 0])
    return jnp.stack([real_part, imag_part])


def rotate(summed, first_bin, advance_offset, period):
    twiddle = angles(first_bin, summed.shape[1], period, advance_offset)[:, :, None]
    cosine = jnp.cos(twiddle)
    sine_part = jnp.sin(twiddle)
    real_part = summed[0] * cosine - summed[1] * sine_part
    imag_part = summed[0] * sine_part + summed[1] * cosine
    return jnp.stack([real_part, imag_part])


def on_device(samples, response_tiles, slot_sensor, sensor_noise, advance_offset):
    highest = lax.Precision.HIGHEST
    bins_dev = response_tiles.shape[0]
    first_bin = lax.axis_index(FREQ) * bins_dev
    period = 2 * KEPT_HARMONICS
    step_count = samples.shape[2]
    live_slot = (slot_sensor >= 0).astype(jnp.bfloat16)
    blocks = response_tiles * live_slot[None, None, :, None]
    sensor_ids = lax.iota(jnp.int32, sensor_noise.shape[0])
    slot_noise = jnp.sum(
        jnp.where(
            slot_sensor[:, None] == sensor_ids[None, :], sensor_noise[None, :], jnp.float32(0.0)
        ),
        axis=1,
    )
    wide = blocks.astype(jnp.float32)
    power = wide[:, 0] * wide[:, 0] + wide[:, 1] * wide[:, 1]
    bin_index = first_bin + lax.iota(jnp.int32, bins_dev)
    bin_weight = jnp.where(bin_index == 0, 1.0, 2.0).astype(jnp.float32) / period
    per_bin = jnp.einsum("ksq,s->kq", power, slot_noise, precision=highest)
    noise_spread = one_axis_at_a_time(jnp.dot(bin_weight, per_bin, precision=highest), FREQ_SENS)
    forward = forward_table(KEPT_HARMONICS, step_count, period)
    spectra = jnp.einsum(
        "rst,ckt->ckrs", samples, forward, preferred_element_type=jnp.float32
    ).astype(jnp.bfloat16)
    partial_value = contract(spectra, collect(blocks, FREQ, 0))
    base_bin = 0
    backward = inverse_table(KEPT_HARMONICS, step_count, period)
    shifted = rotate(partial_value, base_bin, advance_offset, period)
    kept_entries_local = jnp.einsum("ckqr,ckt->rqt", shifted, backward, precision=highest)
    outlook_values = total_of_pieces(kept_entries_local, SENS).astype(jnp.bfloat16)
    return (outlook_values, noise_spread)


def solution(mesh):
    torus = Mesh(mesh.devices.reshape(4, 8, 8, 2), ("freq_0", "freq_1", "sens_0", "sens_1"))
    return jax.shard_map(
        on_device,
        mesh=torus,
        in_specs=(P(FREQ, SENS, None), P(FREQ, None, SENS, None), P(SENS), P(), P()),
        out_specs=(P(FREQ, None, None), P()),
        check_vma=False,
    )
```

profile of v0, /device:TPU:1, one launch (start us, length us, event | category | flops | bytes accessed | tf_op | source)
XLA Modules:
  0.0 199.6 jit_solution(2900247025246310007)
XLA Ops:
  7.2 0.0 copy-start
  7.2 0.7 compare_convert_fusion
  7.9 1.8 fusion.57
  9.7 4.6 %broadcast_bitcast_fusion = bf16[32,14,21,2,40]{4,3,2,1,0:T(2,128)(2,1)} fusion(bf16[14,2,40,21]{2,1,3,0:T(2,128)(2,1)S(1)} %get-tuple-element.9), kind=kLoop, calls=%fused_computation.81 | loop fusion | bytes 1552320
  14.3 12.6 %reshape.192 = bf16[32,2,11760]{2,1,0:T(2,128)(2,1)} reshape(bf16[32,14,21,2,40]{4,3,2,1,0:T(2,128)(2,1)} %broadcast_bitcast_fusion) | data formatting | bytes 3010560
  26.9 13.8 %all-to-all-start = ((bf16[32,2,11760]{2,1,0:T(2,128)(2,1)}), bf16[32,2,11760]{2,1,0:T(2,128)(2,1)}, u32[]{:S(2)}, u32[]{:S(2)}) async-start(bf16[32,2,11760]{2,1,0:T(2,128)(2,1)} %reshape.192), calls=%async_computation | async-start | bytes 3014656 | tf_op jit(solution)/shard_map/all_to_all | solution.py:22
  40.7 0.2 all-gather.3.cloned.1.call-start
  40.9 3.8 %negate_convert_fusion = (bf16[1,448,420]{1,2,0:T(8,128)(2,1)S(1)}, bf16[1,448,420]{1,2,0:T(8,128)(2,1)S(1)}) fusion(), kind=kLoop, calls=%fused_computation.25 | loop fusion | flops 2257920 | bytes 752640 | tf_op jit(solution)/shard_map/convert.1
  44.7 0.0 copy-done
  44.7 0.8 convolution_convert_fusion
  45.6 0.0 copy-start.7
  45.6 0.1 slice_bitcast_fusion.11
  45.7 1.4 copy.45
  47.1 2.0 %copy.46 = bf16[448,16,40]{2,1,0:T(8,128)(2,1)} copy(bf16[448,16,40]{0,2,1:T(8,128)(2,1)S(1)} %get-tuple-element.13) | data formatting | bytes 1146880 | tf_op jit(solution)/shard_map/squeeze | solution.py:68
  49.1 0.0 copy-done.7
  49.1 1.0 fusion.31
  50.1 4.5 %fusion.22 = (f32[1,448,420]{1,2,0:T(8,128)S(1)}, f32[1,448,420]{1,2,0:T(8,128)}) fusion(f32[448]{0:T(512)S(1)} %select_multiply_fusion, f32[448]{0:T(512)S(1)} %fusion.39), kind=kLoop, calls=%fused_computation.32 | loop fusion | flops 2069760 | bytes 1508864 | tf_op jit(solution)/shard_map/mul | solution.py:59
  54.5 21.6 %all-to-all-done = bf16[32,2,11760]{2,1,0:T(2,128)(2,1)} async-done(((bf16[32,2,11760]{2,1,0:T(2,128)(2,1)}), bf16[32,2,11760]{2,1,0:T(2,128)(2,1)}, u32[]{:S(2)}, u32[]{:S(2)}) %all-to-all-start) | async-done | bytes 1505312 | tf_op jit(solution)/shard_map/all_to_all | solution.py:22
  76.1 12.5 %reshape.193 = bf16[32,14,21,2,40]{4,3,2,1,0:T(2,128)(2,1)} reshape(bf16[32,2,11760]{2,1,0:T(2,128)(2,1)} %all-to-all-done) | data formatting | bytes 3010560
  88.6 3.1 %copy.44 = bf16[32,14,2,40,21]{3,4,1,0,2:T(8,128)(2,1)S(1)} copy(bf16[32,14,2,40,21]{3,2,4,1,0:T(2,128)(2,1)} %bitcast.67) | data formatting | bytes 3010560 | tf_op jit(solution)/shard_map/all_to_all | solution.py:22
  91.6 0.0 copy-start.2
  91.6 1.5 fusion.3
  93.2 0.0 copy-done.2
  93.2 1.5 fusion.2
  94.8 1.6 fusion.6
  96.3 2.1 %subtract_bitcast_fusion = (f32[1,448,21,16]{2,3,1,0:T(8,128)S(1)}, f32[1,448,21,16]{2,3,1,0:T(8,128)S(1)}) fusion(f32[448,21,16]{1,2,0:T(8,128)S(1)} %fusion.6, f32[448,21]{1,0:T(8,128)S(1)} %get-tuple-element.15, f32[448,21]{1,0:T(8,128)S(1)} %get-tuple-element.14, f32[448,21,16]{1,2,0:T(8,128)S(1)} %fusion.2, bf16[448,16,40]{2,1,0:T(8,128)(2,1)S(1)} %copy.45, ...), kind=kOutput, calls=%fused_computation.4 | convolution fusion | flops 13095936 | bytes 13590528 | tf_op jit(solution)/shard_map/krs,ksq->kqr/dot_general | solution.py:66
  98.4 0.0 copy-start.3
  98.4 0.5 pad_maximum_fusion
  98.9 0.7 copy-done.3
  99.6 13.8 %fusion.10 = f32[16,21,420]{2,1,0:T(8,128)S(1)} fusion(f32[2,448,21,16]{2,3,1,0:T(8,128)S(1)} %pad_maximum_fusion, f32[1,448,420]{1,2,0:T(8,128)S(1)} %copy-done.3, f32[1,448,420]{1,2,0:T(8,128)S(1)} %get-tuple-element.18), kind=kOutput, calls=%fused_computation.18 | convolution fusion | flops 1517698560 | bytes 3273984 | tf_op jit(solution)/shard_map/ckqr,ckt->rqt/dot_general | solution.py:111
  113.4 1.3 copy.50
  114.7 0.0 all-gather.3.cloned.1.call-update
  114.7 0.0 copy-done.5
  114.7 0.0 copy-done.6
  114.8 0.2 select_reduce_fusion
  114.9 0.0 copy-done.4
  114.9 0.2 fusion.36
  115.2 0.9 fusion.33
  116.1 0.1 convolution_bitcast_fusion
  116.2 6.8 %psum.28 = f32[21]{0:T(128)S(1)} all-reduce(f32[21]{0:T(128)S(1)} %convolution_bitcast_fusion), channel_id=1, replica_groups=mesh['freq_0'=4,'freq_1'=8,'sens_0'=8,'sens_1'=2] {'freq_0'}, use_global_device_ids=true, to_apply=%region_2.3 | all-reduce | flops 21 | bytes 168 | tf_op jit(solution)/shard_map/psum | solution.py:17
  123.0 16.5 %psum.29 = f32[21]{0:T(128)S(1)} all-reduce(f32[21]{0:T(128)S(1)} %psum.28), channel_id=1, replica_groups=mesh['freq_0'=4,'freq_1'=8,'sens_0'=8,'sens_1'=2] {'freq_1'}, use_global_device_ids=true, to_apply=%region_3.4 | all-reduce | flops 21 | bytes 168 | tf_op jit(solution)/shard_map/psum | solution.py:17
  139.5 16.2 %psum.30 = f32[21]{0:T(128)S(1)} all-reduce(f32[21]{0:T(128)S(1)} %psum.29), channel_id=1, replica_groups=mesh['freq_0'=4,'freq_1'=8,'sens_0'=8,'sens_1'=2] {'sens_0'}, use_global_device_ids=true, to_apply=%region_4.5 | all-reduce | flops 21 | bytes 168 | tf_op jit(solution)/shard_map/psum | solution.py:17
  155.7 10.2 %psum.31 = f32[21]{0:T(128)} all-reduce(f32[21]{0:T(128)S(1)} %psum.30), channel_id=1, replica_groups=mesh['freq_0'=4,'freq_1'=8,'sens_0'=8,'sens_1'=2] {'sens_1'}, use_global_device_ids=true, to_apply=%region_5.6 | all-reduce | flops 21 | bytes 168 | tf_op jit(solution)/shard_map/psum | solution.py:17
  165.9 20.1 %all-gather.3.cloned.1.call-done = f32[256,21,420]{2,0,1:T(8,128)} async-done(((f32[16,21,420]{2,0,1:T(8,128)}), f32[256,21,420]{2,0,1:T(8,128)}) %all-gather.3.cloned.1.call-update) | async-done | bytes 9031696 | tf_op jit(solution)/shard_map/all_gather | solution.py:39
  186.1 5.6 %reduce_sum.18 = bf16[16,21,420]{2,0,1:T(8,128)(2,1)S(1)} reduce(f32[16,16,21,420]{3,1,0,2:T(8,128)} %bitcast.68, f32[]{:T(128)} %constant.47.clone.1), dimensions={0}, to_apply=%region_0.1 | reduce | flops 2116800 | bytes 9313924 | tf_op jit(solution)/shard_map/reduce_sum | solution.py:40
  191.7 0.2 copy.71
  191.9 0.8 copy.52
  192.7 0.0 copy-done.1
  (6 shorter events, 0.0 us)
Async XLA Ops:
  7.2 37.6 %copy-start = (bf16[16,40,420]{2,1,0:T(8,128)(2,1)S(1)}, bf16[16,40,420]{2,1,0:T(8,128)(2,1)}, u32[]{:S(2)}) copy-start(bf16[16,40,420]{2,1,0:T(8,128)(2,1)} %param.5) | copy-start | bytes 1612804
  26.9 49.2 %all-to-all-start = ((bf16[32,2,11760]{2,1,0:T(2,128)(2,1)}), bf16[32,2,11760]{2,1,0:T(2,128)(2,1)}, u32[]{:S(2)}, u32[]{:S(2)}) async-start(bf16[32,2,11760]{2,1,0:T(2,128)(2,1)} %reshape.192), calls=%async_computation | async-start | bytes 3014656 | tf_op jit(solution)/shard_map/all_to_all | solution.py:22
  40.7 145.3 %all-gather.3.cloned.1.call-start = ((), (), s32[]{:S(2)}) async-start(), calls=%async_computation.1 | async-start | bytes 11698176 | tf_op jit(solution)/shard_map/all_gather | solution.py:39
  45.6 3.5 %copy-start.7 = (s32[21]{0:T(128)S(1)}, s32[21]{0:T(128)}, u32[]{:S(2)}) copy-start(s32[21]{0:T(128)} %param.9) | copy-start | bytes 256
  91.6 1.6 copy-start.2
  98.4 1.2 copy-start.3
  99.6 15.2 %copy-start.5 = (f32[600]{0:T(1024)S(1)}, f32[600]{0:T(1024)}, u32[]{:S(2)}) copy-start(f32[600]{0:T(1024)} %param.8) | copy-start | bytes 7204
  99.6 15.2 %copy-start.6 = (s32[40]{0:T(128)S(1)}, s32[40]{0:T(128)}, u32[]{:S(2)}) copy-start(s32[40]{0:T(128)} %param.7) | copy-start | bytes 484
  99.6 15.4 %copy-start.4 = (f32[14,2,40,21]{2,1,3,0:T(2,128)S(1)}, f32[14,2,40,21]{2,1,3,0:T(2,128)}, u32[]{:S(2)}) copy-start(f32[14,2,40,21]{2,1,3,0:T(2,128)} %get-tuple-element.8) | copy-start | bytes 282244
  186.1 6.7 %copy-start.1 = (bf16[16,40,420]{2,1,0:T(8,128)(2,1)S(1)}, bf16[16,40,420]{2,1,0:T(8,128)(2,1)}, u32[]{:S(2)}) copy-start(bf16[16,40,420]{2,1,0:T(8,128)(2,1)} %param.5) | copy-start | bytes 1612804
Sparse Core Ops, SparseCore 0:
  114.8 71.1 all-gather.2
where the time goes:
time: 200 us
  blocking collectives  49.7 us (25%)
  waiting for transfers between devices  41.7 us (21%)
  local copies, waits for them, and re-layouts  39.2 us (20%)
  matrix products  22.5 us (11%)
  other arithmetic  18.2 us (9%)
  between operations  14.2 us (7%)
  starting transfers between devices  14 us (7%)
    psum x4, blocking collectives, one_axis_at_a_time(): return functools.reduce(lax.psum, axes, array)  49.7 us
    unnamed x21, local copies, waits for them, and re-layouts  31.4 us
    all_to_all x1, waiting for transfers between devices, copy_for_each(): lax.all_to_all(jnp.broadcast_to(array[None], (devices, *array.shape)), ax...  21.6 us
    all_gather x1, waiting for transfers between devices, total_of_pieces(): blocks = lax.all_gather(array, axis)  20.1 us
    dot_general x1, matrix products, on_device(): jnp.einsum('ckqr,ckt->rqt', shifted, backward, precision=highest)  13.8 us
    all_to_all x1, starting transfers between devices, copy_for_each(): lax.all_to_all(jnp.broadcast_to(array[None], (devices, *array.shape)), ax...  13.8 us
    dot_general x4, matrix products, product(): jnp.einsum('krs,ksq->kqr', left, right, preferred_element_type=jnp.float32)  6.73 us
    reduce_sum x1, other arithmetic, total_of_pieces(): return blocks.sum(axis=0)  5.63 us
  transfers between devices with their start and end apart: 2, of which 2 were waited for; matrix products, arithmetic and copies ran while one was open for 8% of the time, Pallas kernels for 0%

commit v1 on v0

v1 whole, which is shorter than its diff:
```python
import math

import jax
import jax.numpy as jnp
import numpy as np
from jax import lax
from jax.sharding import Mesh
from jax.sharding import PartitionSpec as P

KEPT = 448
PERIOD = 2 * KEPT
X, Z, Y, C = "freq_0", "freq_1", "sens_0", "sens_1"
FREQ = (X, Z)
SENS = (Y, C)


def turns(bins, steps):
    k = np.arange(bins)[:, None]
    t = np.arange(steps)[None, :]
    return ((k * t) % PERIOD) * (2.0 * np.pi / PERIOD)


def forward_np(steps):
    a = turns(KEPT, steps)
    return np.stack([np.cos(a), -np.sin(a)])


def inverse_np(steps):
    a = turns(KEPT, steps)
    w = np.where(np.arange(KEPT) == 0, 1.0, 2.0)[:, None] / PERIOD
    return np.stack([w * np.cos(a), -w * np.sin(a)])


def share(array, axis):
    n = lax.axis_size(axis)
    return lax.all_to_all(
        jnp.broadcast_to(array[None], (n, *array.shape)), axis, 0, 0, tiled=True
    )


def three(v):
    hi = v.astype(jnp.bfloat16)
    r = v - hi.astype(jnp.float32)
    mid = r.astype(jnp.bfloat16)
    lo = (r - mid.astype(jnp.float32)).astype(jnp.bfloat16)
    return jnp.stack([hi, mid, lo])


def on_device(samples, response, slot_sensor, sensor_noise, advance_offset):
    f32, bf16 = jnp.float32, jnp.bfloat16
    rows, slots, steps = samples.shape
    bins, _, _, sites = response.shape
    first_bin = lax.axis_index(FREQ) * bins
    live = slot_sensor >= 0
    blocks = jnp.where(live[None, None, :, None], response, 0)
    ids = lax.iota(jnp.int32, sensor_noise.shape[0])
    slot_noise = jnp.sum(
        jnp.where(slot_sensor[:, None] == ids[None, :], sensor_noise[None, :], 0.0), axis=1
    )
    wide = blocks.astype(f32)
    k_own = first_bin + lax.iota(jnp.int32, bins)
    weight = jnp.where(k_own == 0, 1.0, 2.0).astype(f32) / PERIOD
    noise_own = jnp.sum(
        wide * wide * slot_noise[None, None, :, None] * weight[:, None, None, None], axis=(0, 1, 2)
    )
    flat = blocks.transpose(3, 0, 1, 2).reshape(sites, bins * 2 * slots)
    tiles = -(-bins * 2 * slots // 128)
    flat = jnp.pad(flat, ((0, 0), (0, tiles * 128 - flat.shape[1])))
    flat = flat.reshape(sites, tiles, 128).transpose(1, 0, 2).reshape(tiles * sites, 128)
    extra = jnp.pad(three(noise_own), ((0, 0), (0, 128 - sites)))
    payload = jnp.concatenate([flat, extra], axis=0)
    gathered = share(share(payload, Z), X)
    gathered = gathered.reshape(-1, tiles * sites + 3, 128)

    forward = jnp.asarray(forward_np(steps), bf16)
    spectra = jnp.einsum("rst,ckt->ckrs", samples, forward, preferred_element_type=f32)
    spectra = spectra.astype(bf16)
    sre, sim = spectra[0], spectra[1]
    left = jnp.stack(
        [jnp.concatenate([sre, -sim], axis=2), jnp.concatenate([sim, sre], axis=2)], axis=1
    ).reshape(KEPT, 2 * rows, 2 * slots)

    noise_freq = jnp.sum(gathered[:, tiles * sites :, :sites].astype(f32), axis=(0, 1))
    blk = gathered[:, : tiles * sites].reshape(-1, tiles, sites, 128).transpose(0, 2, 1, 3)
    blk = blk.reshape(-1, sites, tiles * 128)[:, :, : bins * 2 * slots]
    blk = blk.reshape(-1, sites, bins, 2 * slots).transpose(0, 2, 1, 3)
    blk = blk.reshape(KEPT, sites, 2 * slots)
    zc = jnp.einsum("kns,kqs->knq", left, blk, preferred_element_type=f32)
    zc = zc.reshape(KEPT, 2, rows, sites)
    k_all = lax.iota(jnp.int32, KEPT)
    turn = (k_all[:, None] * advance_offset[None, :]) % PERIOD
    ang = turn.astype(f32) * (2.0 * math.pi / PERIOD)
    cos, sin = jnp.cos(ang)[:, None, :], jnp.sin(ang)[:, None, :]
    z0, z1 = zc[:, 0], zc[:, 1]
    shifted = jnp.stack([z0 * cos - z1 * sin, z0 * sin + z1 * cos]).astype(bf16)
    backward = jnp.asarray(inverse_np(steps), bf16)
    part = jnp.einsum("ckrq,ckt->rqt", shifted, backward, preferred_element_type=f32)
    lanes = -(-(steps + 3) // 128) * 128
    tail = three(noise_freq).T
    tail = jnp.broadcast_to(tail[None], (rows, sites, 3))
    piece = jnp.concatenate(
        [part.astype(bf16), tail, jnp.zeros((rows, sites, lanes - steps - 3), bf16)], axis=2
    )
    got = lax.all_to_all(piece, SENS, 0, 0, tiled=True)
    total = jnp.sum(got.astype(f32), axis=0)
    noise_spread = jnp.sum(total[:, steps : steps + 3], axis=1)
    own = total.astype(bf16)
    outlook = share(own, SENS)[:, :, :steps]
    return outlook, noise_spread


def solution(mesh):
    torus = Mesh(mesh.devices.reshape(4, 8, 8, 2), (X, Z, Y, C))
    return jax.shard_map(
        on_device,
        mesh=torus,
        in_specs=(P(FREQ, SENS, None), P(FREQ, None, SENS, None), P(SENS), P(), P()),
        out_specs=(P(FREQ, None, None), P()),
        check_vma=False,
    )
```

time: 200 us -> 119 us (0.59)
  matrix products: 22.5 us -> 5.96 us
  local copies, waits for them, and re-layouts: 39.2 us -> 22.9 us
  waiting for transfers between devices: 41.7 us -> 26.3 us
  between operations: 14.2 us -> 0.92 us
  other arithmetic: 18.2 us -> 6.33 us
  starting transfers between devices: 14 us -> 7.78 us
    psum x4 -> x0, blocking collectives: 49.7 us -> none  [one_axis_at_a_time(): return functools.reduce(lax.psum, axes, array)]
    all_to_all x0 -> x2, blocking collectives: none -> 48.5 us  [the longest x1 24.3 us: on_device(): got = lax.all_to_all(piece, SENS, 0, 0, tiled=True)]
    unnamed x21 -> x11, local copies, waits for them, and re-layouts: 31.4 us -> 0.87 us
    all_gather x1 -> x0, waiting for transfers between devices: 20.1 us -> none  [total_of_pieces(): blocks = lax.all_gather(array, axis)]
    dot_general x8 -> x3, matrix products: 22.5 us -> 5.96 us  [the longest x1 4.53 us: on_device(): zc = jnp.einsum('kns,kqs->knq', left, blk, preferred_element_type=f32)]
    reshape x0 -> x7, local copies, waits for them, and re-layouts: none -> 14.6 us  [the longest x1 4.64 us: on_device(): zc = zc.reshape(KEPT, 2, rows, sites)]
    all_to_all x1 -> x2, starting transfers between devices: 13.8 us -> 7.78 us  [share(): lax.all_to_all(jnp.broadcast_to(array[None], (n, *array.shape)), axis, 0,...]
    all_to_all x1 -> x2, waiting for transfers between devices: 21.6 us -> 26.3 us  [share(): lax.all_to_all(jnp.broadcast_to(array[None], (n, *array.shape)), axis, 0,...]
  transfers between devices with their start and end apart: 2 -> 2, of which waited for: 2 -> 2; matrix products, arithmetic and copies ran while one was open for 8% -> 5% of each run, Pallas kernels for 0% -> 0%
where the time goes in v1:
time: 119 us
  blocking collectives  48.5 us (41%)
  waiting for transfers between devices  26.3 us (22%)
  local copies, waits for them, and re-layouts  22.9 us (19%)
  starting transfers between devices  7.78 us (7%)
  other arithmetic  6.33 us (5%)
  matrix products  5.96 us (5%)
    all_to_all x2, waiting for transfers between devices, share(): lax.all_to_all(jnp.broadcast_to(array[None], (n, *array.shape)), axis, 0,...  26.3 us
    all_to_all x1, blocking collectives, on_device(): got = lax.all_to_all(piece, SENS, 0, 0, tiled=True)  24.3 us
    all_to_all x1, blocking collectives, share(): lax.all_to_all(jnp.broadcast_to(array[None], (n, *array.shape)), axis, 0,...  24.2 us
    all_to_all x2, starting transfers between devices, share(): lax.all_to_all(jnp.broadcast_to(array[None], (n, *array.shape)), axis, 0,...  7.78 us
    reshape x1, local copies, waits for them, and re-layouts, on_device(): zc = zc.reshape(KEPT, 2, rows, sites)  4.64 us
    reshape x1, local copies, waits for them, and re-layouts, on_device(): blk = blk.reshape(-1, sites, bins, 2 * slots).transpose(0, 2, 1, 3)  4.63 us
    dot_general x1, matrix products, on_device(): zc = jnp.einsum('kns,kqs->knq', left, blk, preferred_element_type=f32)  4.53 us
    reshape x1, local copies, waits for them, and re-layouts, on_device(): left = jnp.stack([jnp.concatenate([sre, -sim], axis=2), jnp.concatenate([...  3.58 us
  transfers between devices with their start and end apart: 2, of which 2 were waited for; matrix products, arithmetic and copies ran while one was open for 5% of the time, Pallas kernels for 0%

profile of v1, /device:TPU:1, one launch (start us, length us, event | category | flops | bytes accessed | tf_op | source)
XLA Modules:
  0.0 118.7 jit_solution(6149441194009599474)
XLA Ops:
  0.6 0.0 copy-start
  0.7 0.7 broadcast_compare_fusion
  1.4 0.9 select_reduce_fusion
  2.3 1.4 %multiply_reduce_fusion = f32[21]{0:T(128)S(1)} fusion(f32[14]{0:T(128)S(1)} %fusion.18, f32[40]{0:T(128)S(1)} %select_reduce_fusion, bf16[14,2,40,21]{2,1,3,0:T(2,128)(2,1)} %param.8, pred[40]{0:T(512)(128)(4,1)S(1)} %broadcast_compare_fusion), kind=kLoop, calls=%fused_computation.20 | loop fusion | flops 141099 | bytes 47380 | tf_op jit(solution)/shard_map/reduce_sum | solution.py:63
  3.7 1.0 fusion.5
  4.7 0.1 copy.34
  4.8 0.3 reshape.204
  5.1 0.1 reshape.205
  5.3 0.1 broadcast_in_dim.75
  5.4 24.2 %all_to_all.20 = bf16[8,192,128]{2,1,0:T(8,128)(2,1)S(1)} all-to-all(bf16[8,192,128]{2,1,0:T(8,128)(2,1)S(1)} %broadcast_in_dim.75), channel_id=1, replica_groups=mesh['freq_0'=4,'freq_1'=8,'sens_0'=8,'sens_1'=2] {'freq_1'}, dimensions={0} | all-to-all | bytes 786432 | tf_op jit(solution)/shard_map/all_to_all | solution.py:36
  29.6 0.3 copy.36
  29.8 0.0 copy-start.4
  29.9 1.4 %broadcast_in_dim.76 = bf16[4,8,192,128]{3,1,2,0:T(8,128)(2,1)} broadcast(bf16[8,192,128]{2,0,1:T(8,128)(2,1)S(1)} %copy.36), dimensions={1,2,3} | broadcast | bytes 1966080 | tf_op jit(solution)/shard_map/broadcast_in_dim | solution.py:37
  31.3 4.3 %all-to-all-start.1 = ((bf16[4,8,192,128]{3,1,2,0:T(8,128)(2,1)}), bf16[4,8,192,128]{3,1,2,0:T(8,128)(2,1)}, u32[]{:S(2)}, u32[]{:S(2)}) async-start(bf16[4,8,192,128]{3,1,2,0:T(8,128)(2,1)} %broadcast_in_dim.76), calls=%async_computation.1 | async-start | bytes 3145728 | tf_op jit(solution)/shard_map/all_to_all | solution.py:36
  35.6 0.0 copy-done
  35.6 0.0 copy-done.4
  35.6 0.8 convolution_convert_fusion
  36.5 0.1 slice_bitcast_fusion.2
  36.6 0.4 maximum_bitcast_fusion
  37.0 0.3 pad_maximum_fusion
  37.4 0.0 copy-start.2
  37.4 3.6 %copy.40 = bf16[448,32,80]{2,1,0:T(8,128)(2,1)} copy(bf16[448,32,80]{0,2,1:T(8,128)(2,1)S(1)} %bitcast.91) | data formatting | bytes 4587520 | tf_op jit(solution)/shard_map/reshape | solution.py:81
  41.0 0.1 pad.12.clone
  41.1 0.0 copy-done.2
  41.1 0.3 fusion.11
  41.4 13.1 %all-to-all-done.1 = bf16[4,8,192,128]{3,1,2,0:T(8,128)(2,1)} async-done(((bf16[4,8,192,128]{3,1,2,0:T(8,128)(2,1)}), bf16[4,8,192,128]{3,1,2,0:T(8,128)(2,1)}, u32[]{:S(2)}, u32[]{:S(2)}) %all-to-all-start.1) | async-done | bytes 1572896 | tf_op jit(solution)/shard_map/all_to_all | solution.py:36
  54.4 1.7 %copy.53 = bf16[4,8,192,128]{3,1,0,2:T(8,128)(2,1)S(1)} copy(bf16[4,8,192,128]{3,1,2,0:T(8,128)(2,1)} %all-to-all-done.1) | data formatting | bytes 3145728 | tf_op jit(solution)/shard_map/all_to_all | solution.py:36
  56.1 0.3 slice.38
  56.4 0.1 copy.44
  56.5 1.4 %copy.54 = bf16[9,21,4,8,128]{4,3,0,2,1:T(8,128)(2,1)} copy(bf16[9,21,4,8,128]{4,3,2,1,0:T(8,128)(2,1)S(1)} %bitcast.95) | data formatting | bytes 3096576 | tf_op jit(solution)/shard_map/reshape | solution.py:85
  58.0 4.6 %reshape.210 = bf16[32,21,14,80]{3,2,0,1:T(8,128)(2,1)S(1)} reshape(bf16[32,21,1120]{2,0,1:T(8,128)(2,1)} %bitcast.96) | data formatting | bytes 3010560 | tf_op jit(solution)/shard_map/reshape | solution.py:86
  62.6 0.0 copy-start.1
  62.6 2.5 %copy.39 = bf16[32,14,21,80]{3,2,1,0:T(8,128)(2,1)S(1)} copy(bf16[32,14,21,80]{3,1,0,2:T(8,128)(2,1)S(1)} %bitcast.90) | data formatting | bytes 3010560 | tf_op jit(solution)/shard_map/transpose | solution.py:86
  65.2 0.0 copy-done.1
  65.2 4.5 %fusion.23 = f32[448,32,21]{1,2,0:T(8,128)} fusion(bf16[448,32,80]{2,1,0:T(8,128)(2,1)S(1)} %copy-done.1, bf16[448,21,80]{2,1,0:T(8,128)(2,1)S(1)} %bitcast.89), kind=kOutput, calls=%fused_computation.57 | convolution fusion | flops 48168960 | bytes 5003264 | tf_op jit(solution)/shard_map/kns,kqs->knq/dot_general | solution.py:88
  69.7 0.0 copy-start.3
  69.7 4.6 %copy.48 = f32[448,32,21]{0,2,1:T(8,128)S(1)} copy(f32[448,32,21]{1,2,0:T(8,128)} %fusion.23) | data formatting | bytes 2408448 | tf_op jit(solution)/shard_map/reshape | solution.py:89
  74.3 0.2 subtract_convert_fusion
  74.6 0.0 copy-done.3
  74.6 0.6 fusion
  75.2 0.1 maximum_maximum_fusion
  75.3 24.3 %all_to_all.21 = bf16[16,21,512]{2,1,0:T(8,128)(2,1)S(1)} all-to-all(bf16[16,21,512]{2,1,0:T(8,128)(2,1)S(1)} %maximum_maximum_fusion), channel_id=1, replica_groups=mesh['freq_0'=4,'freq_1'=8,'sens_0'=8,'sens_1'=2] {'sens_0','sens_1'}, dimensions={0} | all-to-all | bytes 688128 | tf_op jit(solution)/shard_map/all_to_all | solution.py:104
  99.7 0.1 convert_reduce_fusion
  99.7 0.8 broadcast_in_dim.79
  100.5 3.4 %all-to-all-start.3 = ((bf16[16,21,512]{2,1,0:T(8,128)(2,1)}), bf16[16,21,512]{2,1,0:T(8,128)(2,1)S(1)}, u32[]{:S(2)}, u32[]{:S(2)}) async-start(bf16[16,21,512]{2,1,0:T(8,128)(2,1)} %broadcast_in_dim.79), calls=%async_computation.3 | async-start | bytes 786432 | tf_op jit(solution)/shard_map/all_to_all | solution.py:36
  104.0 0.7 slice_reduce_fusion
  104.7 13.2 %all-to-all-done.3 = bf16[16,21,512]{2,1,0:T(8,128)(2,1)S(1)} async-done(((bf16[16,21,512]{2,1,0:T(8,128)(2,1)}), bf16[16,21,512]{2,1,0:T(8,128)(2,1)S(1)}, u32[]{:S(2)}, u32[]{:S(2)}) %all-to-all-start.3) | async-done | bytes 344096 | tf_op jit(solution)/shard_map/all_to_all | solution.py:36
  117.9 0.8 copy.45
  (16 shorter events, 0.2 us)
Async XLA Ops:
  0.6 35.0 %copy-start = (bf16[16,40,420]{2,1,0:T(8,128)(2,1)S(1)}, bf16[16,40,420]{2,1,0:T(8,128)(2,1)}, u32[]{:S(2)}) copy-start(bf16[16,40,420]{2,1,0:T(8,128)(2,1)} %param.7) | copy-start | bytes 1612804
  29.8 5.8 %copy-start.4 = (bf16[2,448,420,1]{1,2,3,0:T(8,128)(2,1)S(1)}, bf16[2,448,420,1]{1,2,3,0:T(8,128)(2,1)}, u32[]{:S(2)}) copy-start(bf16[2,448,420,1]{1,2,3,0:T(8,128)(2,1)} %constant.57) | copy-start | bytes 2257924
  31.3 23.1 %all-to-all-start.1 = ((bf16[4,8,192,128]{3,1,2,0:T(8,128)(2,1)}), bf16[4,8,192,128]{3,1,2,0:T(8,128)(2,1)}, u32[]{:S(2)}, u32[]{:S(2)}) async-start(bf16[4,8,192,128]{3,1,2,0:T(8,128)(2,1)} %broadcast_in_dim.76), calls=%async_computation.1 | async-start | bytes 3145728 | tf_op jit(solution)/shard_map/all_to_all | solution.py:36
  37.4 3.7 %copy-start.2 = (s32[21]{0:T(128)S(1)}, s32[21]{0:T(128)}, u32[]{:S(2)}) copy-start(s32[21]{0:T(128)} %param.11) | copy-start | bytes 256
  62.6 2.6 %copy-start.1 = (bf16[448,32,80]{2,1,0:T(8,128)(2,1)S(1)}, bf16[448,32,80]{2,1,0:T(8,128)(2,1)}, u32[]{:S(2)}) copy-start(bf16[448,32,80]{2,1,0:T(8,128)(2,1)} %copy.40) | copy-start | bytes 6881284
  69.7 4.9 %copy-start.3 = (bf16[2,448,420,1]{1,2,0,3:T(8,128)(2,1)S(1)}, bf16[2,448,420,1]{1,2,0,3:T(8,128)(2,1)}, u32[]{:S(2)}) copy-start(bf16[2,448,420,1]{1,2,0,3:T(8,128)(2,1)} %constant.58) | copy-start | bytes 2257924
  100.5 17.4 %all-to-all-start.3 = ((bf16[16,21,512]{2,1,0:T(8,128)(2,1)}), bf16[16,21,512]{2,1,0:T(8,128)(2,1)S(1)}, u32[]{:S(2)}, u32[]{:S(2)}) async-start(bf16[16,21,512]{2,1,0:T(8,128)(2,1)} %broadcast_in_dim.79), calls=%async_computation.3 | async-start | bytes 786432 | tf_op jit(solution)/shard_map/all_to_all | solution.py:36

commit v2 on v1

v2 whole, which is shorter than its diff:
```python
import functools
import math

import jax
import jax.numpy as jnp
import numpy as np
from jax import lax
from jax.experimental import pallas as pl
from jax.experimental.pallas import tpu as pltpu
from jax.sharding import Mesh
from jax.sharding import PartitionSpec as P

KEPT = 448
PERIOD = 2 * KEPT
BINS, SLOTS, SITES, STEPS, ROWS = 14, 40, 21, 420, 16
SOURCES = KEPT // BINS
CHUNKS, HALVES = 6, 5
DEPTH = HALVES * SLOTS
TALL = SOURCES * CHUNKS * 8
WIDE = 512
X, Z, Y, C = "freq_0", "freq_1", "sens_0", "sens_1"
FREQ = (X, Z)
SENS = (Y, C)
f32, bf16 = jnp.float32, jnp.bfloat16
PLAIN = (((1,), (0,)), ((), ()))


def base_table():
    k = np.arange(KEPT)[:, None]
    t = np.arange(STEPS)[None, :]
    a = ((k * t) % PERIOD) * (2.0 * np.pi / PERIOD)
    return np.stack([np.cos(a), -np.sin(a)], axis=1)


def chunk_rows(table):
    table = table.reshape(SOURCES, BINS, 2, STEPS)
    table = jnp.pad(table, ((0, 0), (0, 2), (0, 0), (0, WIDE - STEPS)))
    parts = [table[:, 5 * g // 2 : 5 * g // 2 + 4] for g in range(CHUNKS)]
    return jnp.stack(parts, axis=1)


def chunk_mask():
    mask = np.zeros((CHUNKS, 8, 256), np.float32)
    for g in range(CHUNKS):
        for h in range(HALVES):
            if 5 * g + h < 2 * BINS:
                b = (5 * g + h) // 2 - 5 * g // 2
                mask[g, 2 * b : 2 * b + 2, h * SLOTS : (h + 1) * SLOTS] = 1.0
    return mask.reshape(CHUNKS * 8, 256)


def spread_kernel(xa_ref, xb_ref, ta_ref, tb_ref, mask_ref, out_ref):
    dims = (((1,), (1,)), ((), ()))
    mask = mask_ref[...]
    halves = []
    for j in range(2):
        d = lax.dot_general(ta_ref[...], xa_ref[j], dims, preferred_element_type=f32)
        d += lax.dot_general(tb_ref[...], xb_ref[j], dims, preferred_element_type=f32)
        d = d.reshape(SOURCES, CHUNKS * 8, 256) * mask[None]
        halves.append(d.reshape(SOURCES * CHUNKS, 8, 256))
    both = jnp.concatenate(halves, axis=1).astype(bf16)
    out_ref[...] = both.reshape(SOURCES, CHUNKS, 16, 256)


def spread(samples, forward):
    rows = chunk_rows(forward)
    re, im = rows[..., 0, :], rows[..., 1, :]
    turned = jnp.stack([-im, re], axis=-2)
    even = (jnp.arange(CHUNKS) % 2 == 0)[None, :, None, None, None]
    ta = jnp.where(even, rows, turned).reshape(TALL, WIDE)
    tb = jnp.where(even, turned, rows).reshape(TALL, WIDE)
    x = jnp.pad(samples, ((0, 0), (0, 0), (0, WIDE - STEPS)))
    o = jnp.zeros_like(x)
    e = jnp.zeros((ROWS, 256 - DEPTH, WIDE), bf16)
    xa = jnp.concatenate([x, o, x, o, x, e], axis=1)
    xb = jnp.concatenate([o, x, o, x, o, e], axis=1)
    return pl.pallas_call(
        spread_kernel,
        grid=(ROWS // 2,),
        in_specs=[
            pl.BlockSpec((2, 256, WIDE), lambda p: (p, 0, 0)),
            pl.BlockSpec((2, 256, WIDE), lambda p: (p, 0, 0)),
            pl.BlockSpec((TALL, WIDE), lambda p: (0, 0)),
            pl.BlockSpec((TALL, WIDE), lambda p: (0, 0)),
            pl.BlockSpec((CHUNKS * 8, 256), lambda p: (0, 0)),
        ],
        out_specs=pl.BlockSpec((SOURCES, CHUNKS, 16, 256), lambda p: (0, 0, p, 0)),
        out_shape=jax.ShapeDtypeStruct((SOURCES, CHUNKS, 8 * ROWS, 256), bf16),
        cost_estimate=pl.CostEstimate(
            flops=4 * TALL * WIDE * 256 * ROWS, transcendentals=0, bytes_accessed=30_000_000
        ),
        name="spread",
    )(xa, xb, ta, tb, jnp.asarray(chunk_mask()))


BLOCK = 8


def finish_kernel(left_ref, gath_ref, inv_ref, tail_ref, out_ref, z_ref):
    step = pl.program_id(0)
    lane = lax.broadcasted_iota(jnp.int32, (4, 8, 128), 2)
    for i in range(BLOCK):
        left = left_ref[i].reshape(CHUNKS * 8 * ROWS, 256)[:, :DEPTH]
        prod = lax.dot_general(left, gath_ref[i], PLAIN, preferred_element_type=f32)
        prod = prod.reshape(CHUNKS, 4, 4, 8, 128)
        packed = []
        for g in range(CHUNKS):
            acc = jnp.zeros((4, 8, 128), f32)
            for r in range(4):
                moved = pltpu.roll(prod[g, :, r], (32 * r - SITES * g) % 128, 2)
                acc = jnp.where((lane >= 32 * r) & (lane < 32 * r + SITES), moved, acc)
            packed.append(acc)
        start = pl.multiple_of((step * BLOCK + i) * CHUNKS * 8, 16)
        for q in range(4):
            col = jnp.concatenate([packed[g][q] for g in range(CHUNKS)], axis=0)
            z_ref[pl.ds(start, CHUNKS * 8), 128 * q : 128 * (q + 1)] = col.astype(bf16)

    @pl.when(step == SOURCES // BLOCK - 1)
    def _():
        total = lax.dot_general(inv_ref[...], z_ref[...], PLAIN, preferred_element_type=f32)
        total = total.T * (2.0 / PERIOD)
        total = total.reshape(ROWS, 32, WIDE) + tail_ref[...][None]
        out_ref[...] = total[:, :24].astype(bf16)


def finish(left, gathered, inverse, tail):
    return pl.pallas_call(
        finish_kernel,
        grid=(SOURCES // BLOCK,),
        in_specs=[
            pl.BlockSpec((BLOCK, CHUNKS, 8 * ROWS, 256), lambda p: (p, 0, 0, 0)),
            pl.BlockSpec((BLOCK, DEPTH, 128), lambda p: (p, 0, 0)),
            pl.BlockSpec((WIDE, TALL), lambda p: (0, 0)),
            pl.BlockSpec((32, WIDE), lambda p: (0, 0)),
        ],
        out_specs=pl.BlockSpec((ROWS, 24, WIDE), lambda p: (0, 0, 0)),
        out_shape=jax.ShapeDtypeStruct((ROWS, 24, WIDE), bf16),
        scratch_shapes=[pltpu.VMEM((TALL, 4 * 128), bf16)],
        name="finish",
    )(left, gathered, inverse, tail)


def inverse_of(forward):
    half = jnp.where(jnp.arange(KEPT) == 0, 0.5, 1.0).astype(bf16)
    return chunk_rows(forward * half[:, None, None]).reshape(TALL, WIDE).T


def share(array, axis):
    n = lax.axis_size(axis)
    return lax.all_to_all(
        jnp.broadcast_to(array[None], (n, *array.shape)), axis, 0, 0, tiled=True
    )


def three(v):
    hi = v.astype(bf16)
    r = v - hi.astype(f32)
    mid = r.astype(bf16)
    lo = (r - mid.astype(f32)).astype(bf16)
    return jnp.stack([hi, mid, lo])


def payload_of(response, slot_sensor, sensor_noise, advance_offset, first_bin):
    live = slot_sensor >= 0
    blocks = jnp.where(live[None, None, :, None], response, 0).astype(f32)
    ids = lax.iota(jnp.int32, sensor_noise.shape[0])
    slot_noise = jnp.sum(
        jnp.where(slot_sensor[:, None] == ids[None, :], sensor_noise[None, :], 0.0), axis=1
    )
    k_own = first_bin + lax.iota(jnp.int32, BINS)
    weight = jnp.where(k_own == 0, 1.0, 2.0).astype(f32) / PERIOD
    noise_own = jnp.sum(
        blocks * blocks * slot_noise[None, None, :, None] * weight[:, None, None, None],
        axis=(0, 1, 2),
    )
    turn = (k_own[:, None] * advance_offset[None, :]) % PERIOD
    ang = turn.astype(f32) * (2.0 * math.pi / PERIOD)
    cos, sin = jnp.cos(ang)[:, None, :], jnp.sin(ang)[:, None, :]
    re, im = blocks[:, 0], blocks[:, 1]
    turned = jnp.stack([re * cos - im * sin, re * sin + im * cos], axis=1).astype(bf16)
    half = turned.reshape(2 * BINS, SLOTS, SITES)
    half = jnp.pad(half, ((0, CHUNKS * HALVES - 2 * BINS), (0, 0), (0, 0)))
    half = half.reshape(CHUNKS, DEPTH, SITES).transpose(1, 0, 2).reshape(DEPTH, CHUNKS * SITES)
    side = jnp.pad(three(noise_own), ((0, 0), (0, 64 - SITES))).reshape(192)
    side = jnp.pad(side, (0, 8))[:, None]
    return jnp.concatenate([half, side, jnp.zeros_like(side)], axis=1)


def tail_of(gathered):
    side = jnp.sum(gathered[:, :192, 126].astype(f32), axis=0)
    noise = jnp.sum(side.reshape(3, 64), axis=0)[:SITES]
    return jnp.pad(three(noise).astype(f32), ((SITES, 8), (0, WIDE - SITES)))


def on_device(samples, response, slot_sensor, sensor_noise, advance_offset):
    first_bin = lax.axis_index(FREQ) * BINS
    forward = lax.optimization_barrier(jnp.asarray(base_table(), bf16))
    payload = payload_of(response, slot_sensor, sensor_noise, advance_offset, first_bin)
    gathered = share(share(payload, Z), X).reshape(SOURCES, DEPTH, 128)
    left = spread(samples, forward)
    piece = finish(left, gathered, inverse_of(forward), tail_of(gathered))
    got = lax.all_to_all(piece, SENS, 0, 0, tiled=True)
    total = jnp.sum(got.astype(f32), axis=0)
    noise_spread = jnp.sum(total[SITES:24, :SITES], axis=0)
    outlook = share(total.astype(bf16), SENS)[:, :SITES, :STEPS]
    return outlook, noise_spread


def solution(mesh):
    torus = Mesh(mesh.devices.reshape(4, 8, 8, 2), (X, Z, Y, C))
    return jax.shard_map(
        on_device,
        mesh=torus,
        in_specs=(P(FREQ, SENS, None), P(FREQ, None, SENS, None), P(SENS), P(), P()),
        out_specs=(P(FREQ, None, None), P()),
        check_vma=False,
    )
```

time: 119 us -> 139 us (1.17)
  Pallas kernels: 0 us -> 28.2 us
  blocking collectives: 48.5 us -> 22.8 us
  other arithmetic: 6.33 us -> 22.8 us
  waiting for transfers between devices: 26.3 us -> 13.4 us
  starting transfers between devices: 7.78 us -> 18.3 us
  local copies, waits for them, and re-layouts: 22.9 us -> 32.2 us
  matrix products: 5.96 us -> 0 us
    pallas_call x0 -> x2, Pallas kernels: none -> 28.2 us  [the longest x1 18.4 us: spread(): pl.pallas_call(spread_kernel, grid=(ROWS // 2,), in_specs=[pl.BlockSpec((...]
    all_to_all x1 -> x0, blocking collectives: 24.2 us -> none  [share(): lax.all_to_all(jnp.broadcast_to(array[None], (n, *array.shape)), axis, 0,...]
    unnamed x11 -> x31, local copies, waits for them, and re-layouts: 0.87 us -> 13.9 us
    all_to_all x2 -> x3, waiting for transfers between devices: 26.3 us -> 13.4 us  [share(): lax.all_to_all(jnp.broadcast_to(array[None], (n, *array.shape)), axis, 0,...]
    all_to_all x2 -> x3, starting transfers between devices: 7.78 us -> 18.3 us  [share(): lax.all_to_all(jnp.broadcast_to(array[None], (n, *array.shape)), axis, 0,...]
    reshape x7 -> x6, local copies, waits for them, and re-layouts: 14.6 us -> 4.95 us  [the longest x2 4.58 us: inverse_of(): return chunk_rows(forward * half[:, None, None]).reshape(TALL, WIDE).T]
    another operation x0 -> x7, local copies, waits for them, and re-layouts: none -> 8.34 us  [the longest x4 6.21 us: chunk_rows(): return jnp.stack(parts, axis=1)]
    dot_general x3 -> x0, matrix products: 5.96 us -> none  [the longest x1 4.53 us: on_device(): zc = jnp.einsum('kns,kqs->knq', left, blk, preferred_element_type=f32)]
  transfers between devices with their start and end apart: 2 -> 3, of which waited for: 2 -> 1; matrix products, arithmetic and copies ran while one was open for 5% -> 29% of each run, Pallas kernels for 0% -> 13%
where the time goes in v2:
time: 139 us
  local copies, waits for them, and re-layouts  32.2 us (23%)
  Pallas kernels  28.2 us (20%)
  other arithmetic  22.8 us (16%)
  blocking collectives  22.8 us (16%)
  starting transfers between devices  18.3 us (13%)
  waiting for transfers between devices  13.4 us (10%)
    all_to_all x1, blocking collectives, on_device(): got = lax.all_to_all(piece, SENS, 0, 0, tiled=True)  22.8 us
    pallas_call x1, Pallas kernels, spread(): pl.pallas_call(spread_kernel, grid=(ROWS // 2,), in_specs=[pl.BlockSpec((...  18.4 us
    all_to_all x3, starting transfers between devices, share(): lax.all_to_all(jnp.broadcast_to(array[None], (n, *array.shape)), axis, 0,...  18.3 us
    unnamed x31, local copies, waits for them, and re-layouts  13.9 us
    all_to_all x3, waiting for transfers between devices, share(): lax.all_to_all(jnp.broadcast_to(array[None], (n, *array.shape)), axis, 0,...  13.4 us
    pallas_call x1, Pallas kernels, finish(): pl.pallas_call(finish_kernel, grid=(SOURCES // BLOCK,), in_specs=[pl.Bloc...  9.77 us
    another operation x4, local copies, waits for them, and re-layouts, chunk_rows(): return jnp.stack(parts, axis=1)  6.21 us
    another operation x1, other arithmetic, spread(): turned = jnp.stack([-im, re], axis=-2)  4.85 us
  transfers between devices with their start and end apart: 3, of which 1 were waited for; matrix products, arithmetic and copies ran while one was open for 29% of the time, Pallas kernels for 13%

profile of v2, /device:TPU:1, one launch (start us, length us, event | category | flops | bytes accessed | tf_op | source)
XLA Modules:
  0.0 138.6 jit_solution(3077012485886500057)
XLA Ops:
  0.7 0.7 broadcast_compare_fusion
  1.3 0.9 select_reduce_fusion
  2.2 1.0 fusion
  3.2 1.4 %multiply_reduce_fusion = f32[21]{0:T(128)S(1)} fusion(f32[14]{0:T(128)S(1)} %fusion.20, f32[40]{0:T(128)S(1)} %select_reduce_fusion, bf16[14,2,40,21]{2,1,3,0:T(2,128)(2,1)} %param.8, pred[40]{0:T(512)(128)(4,1)S(1)} %broadcast_compare_fusion), kind=kLoop, calls=%fused_computation.19 | loop fusion | flops 141099 | bytes 47380 | tf_op jit(solution)/shard_map/reduce_sum | solution.py:172
  4.6 0.8 fusion.12
  5.4 0.8 subtract_convert_fusion
  6.2 0.4 pad_maximum_fusion.1
  7.7 0.8 broadcast_in_dim.116
  8.5 10.9 %all-to-all-start = ((bf16[8,200,128]{2,1,0:T(8,128)(2,1)}), bf16[8,200,128]{2,1,0:T(8,128)(2,1)S(1)}, u32[]{:S(2)}, u32[]{:S(2)}) async-start(bf16[8,200,128]{2,1,0:T(8,128)(2,1)} %broadcast_in_dim.116), calls=%async_computation | async-start | bytes 819200 | tf_op jit(solution)/shard_map/all_to_all | solution.py:150
  19.4 0.3 bitcast_dynamic-update-slice_fusion.4
  20.0 0.3 bitcast_dynamic-update-slice_fusion.2
  20.2 0.3 bitcast_dynamic-update-slice_fusion.1
  20.5 0.3 bitcast_dynamic-update-slice_fusion
  21.0 4.5 %slice_negate_fusion = (bf16[32,6,4,1,512]{4,3,2,1,0:T(2,128)(2,1)}, bf16[32,6,4,1,512]{4,3,2,1,0:T(2,128)(2,1)}) fusion(bf16[32,6,4,2,512]{4,3,2,1,0:T(2,128)(2,1)S(1)} %bitcast_dynamic-update-slice_fusion.11), kind=kLoop, calls=%fused_computation.1 | loop fusion | flops 393216 | bytes 3145728 | tf_op jit(solution)/shard_map/neg | solution.py:68
  25.5 2.0 %stack.81 = bf16[1536,512]{1,0:T(8,128)(2,1)} reshape(bf16[32,6,4,2,512]{4,3,2,1,0:T(2,128)(2,1)S(1)} %bitcast_dynamic-update-slice_fusion.11) | data formatting | bytes 3145728 | tf_op jit(solution)/shard_map/stack | solution.py:39
  27.5 0.9 broadcast_dynamic-update-slice_fusion.4
  28.4 0.6 select_convert_fusion
  29.0 4.9 %pad_maximum_fusion = bf16[32,6,4,2,512]{4,3,2,1,0:T(2,128)(2,1)S(1)} fusion(bf16[32,6,4,1,512]{4,3,2,1,0:T(2,128)(2,1)} %get-tuple-element.9, bf16[32,6,4,1,512]{4,3,2,1,0:T(2,128)(2,1)} %get-tuple-element.8), kind=kLoop, calls=%fused_computation.2 | loop fusion | flops 3145728 | bytes 3145728 | tf_op jit(solution)/shard_map/stack | solution.py:68
  33.9 2.0 %stack.83 = bf16[1536,512]{1,0:T(8,128)(2,1)} reshape(bf16[32,6,4,2,512]{4,3,2,1,0:T(2,128)(2,1)S(1)} %pad_maximum_fusion) | data formatting | bytes 3145728 | tf_op jit(solution)/shard_map/stack | solution.py:68
  35.9 0.9 pad_dynamic-update-slice_fusion.2
  36.8 0.9 broadcast_dynamic-update-slice_fusion.3
  37.7 1.0 pad_dynamic-update-slice_fusion.3
  38.7 0.9 broadcast_dynamic-update-slice_fusion.2
  40.0 1.9 %copy-done.4 = bf16[16,256,512]{2,1,0:T(8,128)(2,1)} copy-done((bf16[16,256,512]{2,1,0:T(8,128)(2,1)}, bf16[16,256,512]{2,1,0:T(8,128)(2,1)S(1)}, u32[]{:S(2)}) %copy-start.4) | copy-done | bytes 4194328
  42.0 1.0 broadcast_dynamic-update-slice_fusion.xb_ref
  43.0 1.6 %broadcast_multiply_fusion = bf16[448,2,420]{2,1,0:T(2,128)(2,1)S(1)} fusion(bf16[448,2,420]{2,1,0:T(2,128)(2,1)S(1)} %copy-done, bf16[448]{0:T(512)(128)(2,1)S(1)} %copy-done.5), kind=kLoop, calls=%fused_computation.6 | loop fusion | flops 376320 | bytes 1506176 | tf_op jit(solution)/shard_map/mul | solution.py:145
  44.6 0.9 bitcast_dynamic-update-slice_fusion.10
  45.6 0.9 bitcast_dynamic-update-slice_fusion.9
  46.5 1.0 bitcast_dynamic-update-slice_fusion.8
  47.5 1.0 bitcast_dynamic-update-slice_fusion.7
  48.4 1.0 bitcast_dynamic-update-slice_fusion.6
  49.8 3.2 %broadcast_select_fusion = (bf16[1536,512]{1,0:T(8,128)(2,1)}, bf16[1536,512]{1,0:T(8,128)(2,1)}) fusion(bf16[1536,512]{1,0:T(8,128)(2,1)} %stack.83, bf16[1536,512]{1,0:T(8,128)(2,1)S(1)} %copy-done.3, pred[1536]{0:T(1024)(128)(4,1)S(1)} %broadcast_in_dim.106), kind=kLoop, calls=%fused_computation.3 | loop fusion | flops 1572864 | bytes 6292992 | tf_op jit(solution)/shard_map/jit(_where)/select_n | solution.py:71
  53.1 1.4 %broadcast_in_dim.117 = bf16[4,8,200,128]{3,2,1,0:T(8,128)(2,1)} broadcast(bf16[8,200,128]{2,1,0:T(8,128)(2,1)S(1)} %all-to-all-done), dimensions={1,2,3} | broadcast | bytes 2048000 | tf_op jit(solution)/shard_map/broadcast_in_dim | solution.py:151
  54.5 4.0 %all-to-all-start.1 = ((bf16[4,8,200,128]{3,2,1,0:T(8,128)(2,1)}), bf16[4,8,200,128]{3,2,1,0:T(8,128)(2,1)S(1)}, u32[]{:S(2)}, u32[]{:S(2)}) async-start(bf16[4,8,200,128]{3,2,1,0:T(8,128)(2,1)} %broadcast_in_dim.117), calls=%async_computation.1 | async-start | bytes 3276800 | tf_op jit(solution)/shard_map/all_to_all | solution.py:150
  58.5 0.9 bitcast_dynamic-update-slice_fusion.5
  59.4 3.1 %copy.49 = bf16[32,6,4,2,512]{4,3,2,1,0:T(2,128)(2,1)S(1)} copy(bf16[32,6,4,2,512]{4,3,2,0,1:T(2,128)(2,1)} %bitcast_dynamic-update-slice_fusion.5) | data formatting | bytes 3145728 | tf_op jit(solution)/shard_map/stack | solution.py:39
  62.5 2.0 %reshape.168 = bf16[1536,512]{1,0:T(8,128)(2,1)} reshape(bf16[32,6,4,2,512]{4,3,2,1,0:T(2,128)(2,1)S(1)} %copy.49) | data formatting | bytes 3145728 | tf_op jit(solution)/shard_map/reshape | solution.py:145
  64.5 2.6 %copy.50 = bf16[1536,512]{0,1:T(8,128)(2,1)} copy(bf16[1536,512]{1,0:T(8,128)(2,1)} %reshape.168) | data formatting | bytes 3145728 | tf_op jit(solution)/shard_map/reshape | solution.py:145
  67.1 18.4 %spread.1.left_ref = bf16[32,6,128,256]{3,2,1,0:T(8,128)(2,1)} custom-call(bf16[16,256,512]{2,1,0:T(8,128)(2,1)} %copy-done.4, bf16[16,256,512]{2,1,0:T(8,128)(2,1)} %broadcast_dynamic-update-slice_fusion.xb_ref, bf16[1536,512]{1,0:T(8,128)(2,1)} %get-tuple-element.7.ta_ref, bf16[1536,512]{1,0:T(8,128)(2,1)} %get-tuple-element.6.tb_ref, ...), custom_call_target="tpu_custom_call" | custom-call | flops 12884901888 | bytes 30000000 | tf_op jit(solution)/shard_map/spread/pallas_call | solution.py:77
  85.5 0.7 convert_reduce_fusion
  86.3 0.6 fusion.3.tail_ref
  86.9 9.8 %finish.1 = bf16[16,24,512]{2,1,0:T(8,128)(2,1)} custom-call(bf16[32,6,128,256]{3,2,1,0:T(8,128)(2,1)} %spread.1.left_ref, bf16[32,200,128]{2,1,0:T(8,128)(2,1)} %bitcast.79, bf16[512,1536]{1,0:T(8,128)(2,1)} %bitcast.80, f32[32,512]{1,0:T(8,128)} %fusion.3.tail_ref), custom_call_target="tpu_custom_call" | custom-call | tf_op jit(solution)/shard_map/finish/pallas_call | solution.py:127
  96.7 22.8 %all_to_all.20 = bf16[16,24,512]{2,1,0:T(8,128)(2,1)S(1)} all-to-all(bf16[16,24,512]{2,1,0:T(8,128)(2,1)} %finish.1), channel_id=1, replica_groups=mesh['freq_0'=4,'freq_1'=8,'sens_0'=8,'sens_1'=2] {'sens_0','sens_1'}, dimensions={0} | all-to-all | bytes 786432 | tf_op jit(solution)/shard_map/all_to_all | solution.py:202
  119.6 0.8 broadcast_in_dim.120
  120.4 3.4 %all-to-all-start.3 = ((bf16[16,24,512]{2,1,0:T(8,128)(2,1)}), bf16[16,24,512]{2,1,0:T(8,128)(2,1)S(1)}, u32[]{:S(2)}, u32[]{:S(2)}) async-start(bf16[16,24,512]{2,1,0:T(8,128)(2,1)} %broadcast_in_dim.120), calls=%async_computation.3 | async-start | bytes 786432 | tf_op jit(solution)/shard_map/all_to_all | solution.py:150
  123.8 0.5 slice_reduce_fusion
  124.4 13.4 %all-to-all-done.3 = bf16[16,24,512]{2,1,0:T(8,128)(2,1)S(1)} async-done(((bf16[16,24,512]{2,1,0:T(8,128)(2,1)}), bf16[16,24,512]{2,1,0:T(8,128)(2,1)S(1)}, u32[]{:S(2)}, u32[]{:S(2)}) %all-to-all-start.3) | async-done | bytes 393248 | tf_op jit(solution)/shard_map/all_to_all | solution.py:150
  137.7 0.8 copy.51
  (45 shorter events, 2.4 us)
Async XLA Ops:
  6.7 12.7 %copy-start = (bf16[448,2,420]{2,1,0:T(2,128)(2,1)S(1)}, bf16[448,2,420]{2,1,0:T(2,128)(2,1)}, u32[]{:S(2)}) copy-start(bf16[448,2,420]{2,1,0:T(2,128)(2,1)} %constant.71.clone) | copy-start | bytes 2257924
  8.5 44.5 %all-to-all-start = ((bf16[8,200,128]{2,1,0:T(8,128)(2,1)}), bf16[8,200,128]{2,1,0:T(8,128)(2,1)S(1)}, u32[]{:S(2)}, u32[]{:S(2)}) async-start(bf16[8,200,128]{2,1,0:T(8,128)(2,1)} %broadcast_in_dim.116), calls=%async_computation | async-start | bytes 819200 | tf_op jit(solution)/shard_map/all_to_all | solution.py:150
  33.9 2.0 %copy-start.2 = (bf16[16,40,420]{2,1,0:T(8,128)(2,1)S(1)}, bf16[16,40,420]{2,1,0:T(8,128)(2,1)}, u32[]{:S(2)}) copy-start(bf16[16,40,420]{2,1,0:T(8,128)(2,1)} %param.7) | copy-start | bytes 1612804
  39.8 3.2 %copy-start.5 = (bf16[448]{0:T(512)(128)(2,1)S(1)}, bf16[448]{0:T(512)(128)(2,1)}, u32[]{:S(2)}) copy-start(bf16[448]{0:T(512)(128)(2,1)} %select_convert_fusion) | copy-start | bytes 2692
  40.0 1.9 %copy-start.4 = (bf16[16,256,512]{2,1,0:T(8,128)(2,1)}, bf16[16,256,512]{2,1,0:T(8,128)(2,1)S(1)}, u32[]{:S(2)}) copy-start(bf16[16,256,512]{2,1,0:T(8,128)(2,1)S(1)} %broadcast_dynamic-update-slice_fusion.1.xa_ref) | copy-start | bytes 12582916
  47.5 2.3 %copy-start.3 = (bf16[1536,512]{1,0:T(8,128)(2,1)S(1)}, bf16[1536,512]{1,0:T(8,128)(2,1)}, u32[]{:S(2)}) copy-start(bf16[1536,512]{1,0:T(8,128)(2,1)} %stack.81) | copy-start | bytes 4718596
  54.5 31.0 %all-to-all-start.1 = ((bf16[4,8,200,128]{3,2,1,0:T(8,128)(2,1)}), bf16[4,8,200,128]{3,2,1,0:T(8,128)(2,1)S(1)}, u32[]{:S(2)}, u32[]{:S(2)}) async-start(bf16[4,8,200,128]{3,2,1,0:T(8,128)(2,1)} %broadcast_in_dim.117), calls=%async_computation.1 | async-start | bytes 3276800 | tf_op jit(solution)/shard_map/all_to_all | solution.py:150
  85.5 1.4 %copy-start.1 = (bf16[4,8,200,128]{3,2,1,0:T(8,128)(2,1)}, bf16[4,8,200,128]{3,2,1,0:T(8,128)(2,1)S(1)}, u32[]{:S(2)}) copy-start(bf16[4,8,200,128]{3,2,1,0:T(8,128)(2,1)S(1)} %all-to-all-done.1) | copy-start | bytes 4915204
  120.4 17.4 %all-to-all-start.3 = ((bf16[16,24,512]{2,1,0:T(8,128)(2,1)}), bf16[16,24,512]{2,1,0:T(8,128)(2,1)S(1)}, u32[]{:S(2)}, u32[]{:S(2)}) async-start(bf16[16,24,512]{2,1,0:T(8,128)(2,1)} %broadcast_in_dim.120), calls=%async_computation.3 | async-start | bytes 786432 | tf_op jit(solution)/shard_map/all_to_all | solution.py:150

commit v3 on v2

--- a/solution.py
+++ b/solution.py
@@ -32,11 +32,11 @@
     return np.stack([np.cos(a), -np.sin(a)], axis=1)
 
 
-def chunk_rows(table):
-    table = table.reshape(SOURCES, BINS, 2, STEPS)
-    table = jnp.pad(table, ((0, 0), (0, 2), (0, 0), (0, WIDE - STEPS)))
+def chunk_rows():
+    table = base_table().reshape(SOURCES, BINS, 2, STEPS)
+    table = np.pad(table, ((0, 0), (0, 2), (0, 0), (0, WIDE - STEPS)))
     parts = [table[:, 5 * g // 2 : 5 * g // 2 + 4] for g in range(CHUNKS)]
-    return jnp.stack(parts, axis=1)
+    return np.stack(parts, axis=1).reshape(TALL, WIDE)
 
 
 def chunk_mask():
@@ -49,11 +49,30 @@
     return mask.reshape(CHUNKS * 8, 256)
 
 
-def spread_kernel(xa_ref, xb_ref, ta_ref, tb_ref, mask_ref, out_ref):
+def spread_kernel(x_ref, table_ref, mask_ref, out_ref, inv_ref, ta_ref, tb_ref, xa_ref, xb_ref):
     dims = (((1,), (1,)), ((), ()))
+
+    @pl.when(pl.program_id(0) == 0)
+    def _():
+        rows = table_ref[...]
+        wide = rows.astype(f32).reshape(SOURCES, CHUNKS, 8, WIDE)
+        sub = lax.broadcasted_iota(jnp.int32, wide.shape, 2)
+        turned = jnp.where(sub % 2 == 0, -pltpu.roll(wide, 7, 2), pltpu.roll(wide, 1, 2))
+        odd = lax.broadcasted_iota(jnp.int32, wide.shape, 1) % 2 == 1
+        ta_ref[...] = jnp.where(odd, turned, wide).reshape(TALL, WIDE).astype(bf16)
+        tb_ref[...] = jnp.where(odd, wide, turned).reshape(TALL, WIDE).astype(bf16)
+        first = lax.broadcasted_iota(jnp.int32, (TALL, WIDE), 0) < 2
+        inv_ref[...] = (rows.astype(f32) * jnp.where(first, 0.5, 1.0)).T.astype(bf16)
+        xa_ref[...] = jnp.zeros_like(xa_ref)
+        xb_ref[...] = jnp.zeros_like(xb_ref)
+
     mask = mask_ref[...]
     halves = []
     for j in range(2):
+        x = x_ref[j]
+        for h in range(HALVES):
+            to = xa_ref if h % 2 == 0 else xb_ref
+            to[j, h * SLOTS : (h + 1) * SLOTS, :STEPS] = x
         d = lax.dot_general(ta_ref[...], xa_ref[j], dims, preferred_element_type=f32)
         d += lax.dot_general(tb_ref[...], xb_ref[j], dims, preferred_element_type=f32)
         d = d.reshape(SOURCES, CHUNKS * 8, 256) * mask[None]
@@ -62,35 +81,34 @@
     out_ref[...] = both.reshape(SOURCES, CHUNKS, 16, 256)
 
 
-def spread(samples, forward):
-    rows = chunk_rows(forward)
-    re, im = rows[..., 0, :], rows[..., 1, :]
-    turned = jnp.stack([-im, re], axis=-2)
-    even = (jnp.arange(CHUNKS) % 2 == 0)[None, :, None, None, None]
-    ta = jnp.where(even, rows, turned).reshape(TALL, WIDE)
-    tb = jnp.where(even, turned, rows).reshape(TALL, WIDE)
-    x = jnp.pad(samples, ((0, 0), (0, 0), (0, WIDE - STEPS)))
-    o = jnp.zeros_like(x)
-    e = jnp.zeros((ROWS, 256 - DEPTH, WIDE), bf16)
-    xa = jnp.concatenate([x, o, x, o, x, e], axis=1)
-    xb = jnp.concatenate([o, x, o, x, o, e], axis=1)
+def spread(samples, table):
     return pl.pallas_call(
         spread_kernel,
         grid=(ROWS // 2,),
         in_specs=[
-            pl.BlockSpec((2, 256, WIDE), lambda p: (p, 0, 0)),
-            pl.BlockSpec((2, 256, WIDE), lambda p: (p, 0, 0)),
-            pl.BlockSpec((TALL, WIDE), lambda p: (0, 0)),
+            pl.BlockSpec((2, SLOTS, STEPS), lambda p: (p, 0, 0)),
             pl.BlockSpec((TALL, WIDE), lambda p: (0, 0)),
             pl.BlockSpec((CHUNKS * 8, 256), lambda p: (0, 0)),
         ],
-        out_specs=pl.BlockSpec((SOURCES, CHUNKS, 16, 256), lambda p: (0, 0, p, 0)),
-        out_shape=jax.ShapeDtypeStruct((SOURCES, CHUNKS, 8 * ROWS, 256), bf16),
+        out_specs=[
+            pl.BlockSpec((SOURCES, CHUNKS, 16, 256), lambda p: (0, 0, p, 0)),
+            pl.BlockSpec((WIDE, TALL), lambda p: (0, 0)),
+        ],
+        out_shape=[
+            jax.ShapeDtypeStruct((SOURCES, CHUNKS, 8 * ROWS, 256), bf16),
+            jax.ShapeDtypeStruct((WIDE, TALL), bf16),
+        ],
+        scratch_shapes=[
+            pltpu.VMEM((TALL, WIDE), bf16),
+            pltpu.VMEM((TALL, WIDE), bf16),
+            pltpu.VMEM((2, 256, WIDE), bf16),
+            pltpu.VMEM((2, 256, WIDE), bf16),
+        ],
         cost_estimate=pl.CostEstimate(
             flops=4 * TALL * WIDE * 256 * ROWS, transcendentals=0, bytes_accessed=30_000_000
         ),
         name="spread",
-    )(xa, xb, ta, tb, jnp.asarray(chunk_mask()))
+    )(samples, table, jnp.asarray(chunk_mask()))
 
 
 BLOCK = 8
@@ -140,11 +158,6 @@
     )(left, gathered, inverse, tail)
 
 
-def inverse_of(forward):
-    half = jnp.where(jnp.arange(KEPT) == 0, 0.5, 1.0).astype(bf16)
-    return chunk_rows(forward * half[:, None, None]).reshape(TALL, WIDE).T
-
-
 def share(array, axis):
     n = lax.axis_size(axis)
     return lax.all_to_all(
@@ -194,11 +207,10 @@
 
 def on_device(samples, response, slot_sensor, sensor_noise, advance_offset):
     first_bin = lax.axis_index(FREQ) * BINS
-    forward = lax.optimization_barrier(jnp.asarray(base_table(), bf16))
     payload = payload_of(response, slot_sensor, sensor_noise, advance_offset, first_bin)
     gathered = share(share(payload, Z), X).reshape(SOURCES, DEPTH, 128)
-    left = spread(samples, forward)
-    piece = finish(left, gathered, inverse_of(forward), tail_of(gathered))
+    left, inverse = spread(samples, jnp.asarray(chunk_rows(), bf16))
+    piece = finish(left, gathered, inverse, tail_of(gathered))
     got = lax.all_to_all(piece, SENS, 0, 0, tiled=True)
     total = jnp.sum(got.astype(f32), axis=0)
     noise_spread = jnp.sum(total[SITES:24, :SITES], axis=0)

time: 139 us -> 112 us (0.81)
  local copies, waits for them, and re-layouts: 32.2 us -> 4.08 us
  blocking collectives: 22.8 us -> 49.3 us
  other arithmetic: 22.8 us -> 8.01 us
  starting transfers between devices: 18.3 us -> 7.46 us
    all_to_all x0 -> x1, blocking collectives: none -> 24.3 us  [share(): lax.all_to_all(jnp.broadcast_to(array[None], (n, *array.shape)), axis, 0,...]
    unnamed x31 -> x3, local copies, waits for them, and re-layouts: 13.9 us -> 0.84 us
    all_to_all x3 -> x2, starting transfers between devices: 18.3 us -> 7.46 us  [share(): lax.all_to_all(jnp.broadcast_to(array[None], (n, *array.shape)), axis, 0,...]
    another operation x5 -> x0, local copies, waits for them, and re-layouts: 8.23 us -> none  [the longest x4 6.21 us: chunk_rows(): return jnp.stack(parts, axis=1)]
    another operation x2 -> x1, other arithmetic: 5.65 us -> 0.8 us  [the longest x1 4.85 us: spread(): turned = jnp.stack([-im, re], axis=-2)]
    reshape x2 -> x0, local copies, waits for them, and re-layouts: 4.58 us -> none  [inverse_of(): return chunk_rows(forward * half[:, None, None]).reshape(TALL, WIDE).T]
    neg x1 -> x0, other arithmetic: 4.51 us -> none  [spread(): turned = jnp.stack([-im, re], axis=-2)]
    select_n x1 -> x0, other arithmetic: 3.25 us -> none  [spread(): tb = jnp.where(even, turned, rows).reshape(TALL, WIDE)]
  transfers between devices with their start and end apart: 3 -> 2, of which waited for: 1 -> 1; matrix products, arithmetic and copies ran while one was open for 29% -> 0% of each run, Pallas kernels for 13% -> 17%
where the time goes in v3:
time: 112 us
  blocking collectives  49.3 us (44%)
  Pallas kernels  28.8 us (26%)
  waiting for transfers between devices  13.4 us (12%)
  other arithmetic  8.01 us (7%)
  starting transfers between devices  7.46 us (7%)
  local copies, waits for them, and re-layouts  4.08 us (4%)
    all_to_all x1, blocking collectives, on_device(): got = lax.all_to_all(piece, SENS, 0, 0, tiled=True)  24.9 us
    all_to_all x1, blocking collectives, share(): lax.all_to_all(jnp.broadcast_to(array[None], (n, *array.shape)), axis, 0,...  24.3 us
    pallas_call x1, Pallas kernels, spread(): pl.pallas_call(spread_kernel, grid=(ROWS // 2,), in_specs=[pl.BlockSpec((...  19 us
    all_to_all x2, waiting for transfers between devices, share(): lax.all_to_all(jnp.broadcast_to(array[None], (n, *array.shape)), axis, 0,...  13.4 us
    pallas_call x1, Pallas kernels, finish(): pl.pallas_call(finish_kernel, grid=(SOURCES // BLOCK,), in_specs=[pl.Bloc...  9.77 us
    all_to_all x2, starting transfers between devices, share(): lax.all_to_all(jnp.broadcast_to(array[None], (n, *array.shape)), axis, 0,...  7.46 us
    broadcast_in_dim x3, local copies, waits for them, and re-layouts, share(): jnp.broadcast_to(array[None], (n, *array.shape))  2.27 us
  transfers between devices with their start and end apart: 2, of which 1 were waited for; matrix products, arithmetic and copies ran while one was open for 0% of the time, Pallas kernels for 17%

profile of v3, /device:TPU:1, one launch (start us, length us, event | category | flops | bytes accessed | tf_op | source)
XLA Modules:
  0.0 111.8 jit_solution(16364388366471502181)
XLA Ops:
  0.7 0.7 broadcast_compare_fusion
  1.3 0.9 select_reduce_fusion
  2.2 1.4 %multiply_reduce_fusion = f32[21]{0:T(128)S(1)} fusion(f32[14]{0:T(128)S(1)} %fusion.19, f32[40]{0:T(128)S(1)} %select_reduce_fusion, bf16[14,2,40,21]{2,1,3,0:T(2,128)(2,1)} %param.8, pred[40]{0:T(512)(128)(4,1)S(1)} %broadcast_compare_fusion), kind=kLoop, calls=%fused_computation.2 | loop fusion | flops 141099 | bytes 47380 | tf_op jit(solution)/shard_map/reduce_sum | solution.py:185
  3.6 1.0 fusion
  4.7 0.1 reshape.131
  4.8 0.8 fusion.12
  5.6 0.8 subtract_convert_fusion
  6.4 0.4 pad_maximum_fusion
  6.8 0.1 copy.16
  6.9 0.2 convert_element_type.126
  7.2 0.2 reshape.129
  7.4 0.1 pad.28.clone
  7.5 0.1 maximum_maximum_fusion
  7.6 0.1 copy.18
  7.7 0.1 broadcast_in_dim.74
  7.8 24.3 %all_to_all.20 = bf16[8,200,128]{2,1,0:T(8,128)(2,1)S(1)} all-to-all(bf16[8,200,128]{2,1,0:T(8,128)(2,1)S(1)} %broadcast_in_dim.74), channel_id=1, replica_groups=mesh['freq_0'=4,'freq_1'=8,'sens_0'=8,'sens_1'=2] {'freq_1'}, dimensions={0} | all-to-all | bytes 819200 | tf_op jit(solution)/shard_map/all_to_all | solution.py:163
  32.1 1.4 %broadcast_in_dim.75 = bf16[4,8,200,128]{3,2,1,0:T(8,128)(2,1)} broadcast(bf16[8,200,128]{2,1,0:T(8,128)(2,1)S(1)} %all_to_all.20), dimensions={1,2,3} | broadcast | bytes 2048000 | tf_op jit(solution)/shard_map/broadcast_in_dim | solution.py:164
  33.5 4.0 %all-to-all-start.1 = ((bf16[4,8,200,128]{3,2,1,0:T(8,128)(2,1)}), bf16[4,8,200,128]{3,2,1,0:T(8,128)(2,1)S(1)}, u32[]{:S(2)}, u32[]{:S(2)}) async-start(bf16[4,8,200,128]{3,2,1,0:T(8,128)(2,1)} %broadcast_in_dim.75), calls=%async_computation.1 | async-start | bytes 3276800 | tf_op jit(solution)/shard_map/all_to_all | solution.py:163
  37.5 19.0 %spread.1 = (bf16[32,6,128,256]{3,2,1,0:T(8,128)(2,1)}, bf16[512,1536]{1,0:T(8,128)(2,1)}) custom-call(bf16[16,40,420]{2,1,0:T(8,128)(2,1)} %x_ref.1, bf16[1536,512]{1,0:T(8,128)(2,1)} %constant.50.clone.table_ref, f32[48,256]{1,0:T(8,128)} %constant.51.clone.mask_ref), custom_call_target="tpu_custom_call" | custom-call | flops 12884901888 | bytes 30000000 | tf_op jit(solution)/shard_map/spread/pallas_call | solution.py:85
  56.5 0.0 all-to-all-done.1
  56.6 0.0 copy-start
  56.6 0.7 convert_reduce_fusion
  57.2 0.1 reshape.133
  57.4 0.6 fusion.3.tail_ref
  58.0 0.0 copy-done
  58.0 9.8 %finish.1 = bf16[16,24,512]{2,1,0:T(8,128)(2,1)} custom-call(bf16[32,6,128,256]{3,2,1,0:T(8,128)(2,1)} %get-tuple-element.4.left_ref, bf16[32,200,128]{2,1,0:T(8,128)(2,1)} %bitcast.30, bf16[512,1536]{1,0:T(8,128)(2,1)} %get-tuple-element.5.inv_ref, f32[32,512]{1,0:T(8,128)} %fusion.3.tail_ref), custom_call_target="tpu_custom_call" | custom-call | tf_op jit(solution)/shard_map/finish/pallas_call | solution.py:145
  67.8 24.9 %all_to_all.21 = bf16[16,24,512]{2,1,0:T(8,128)(2,1)S(1)} all-to-all(bf16[16,24,512]{2,1,0:T(8,128)(2,1)} %finish.1), channel_id=1, replica_groups=mesh['freq_0'=4,'freq_1'=8,'sens_0'=8,'sens_1'=2] {'sens_0','sens_1'}, dimensions={0} | all-to-all | bytes 786432 | tf_op jit(solution)/shard_map/all_to_all | solution.py:214
  92.7 0.1 convert_reduce_fusion.1
  92.8 0.8 broadcast_in_dim.76
  93.6 3.4 %all-to-all-start.3 = ((bf16[16,24,512]{2,1,0:T(8,128)(2,1)}), bf16[16,24,512]{2,1,0:T(8,128)(2,1)S(1)}, u32[]{:S(2)}, u32[]{:S(2)}) async-start(bf16[16,24,512]{2,1,0:T(8,128)(2,1)} %broadcast_in_dim.76), calls=%async_computation.3 | async-start | bytes 786432 | tf_op jit(solution)/shard_map/all_to_all | solution.py:163
  97.0 0.5 slice_reduce_fusion
  97.5 13.4 %all-to-all-done.3 = bf16[16,24,512]{2,1,0:T(8,128)(2,1)S(1)} async-done(((bf16[16,24,512]{2,1,0:T(8,128)(2,1)}), bf16[16,24,512]{2,1,0:T(8,128)(2,1)S(1)}, u32[]{:S(2)}, u32[]{:S(2)}) %all-to-all-start.3) | async-done | bytes 393248 | tf_op jit(solution)/shard_map/all_to_all | solution.py:163
  110.9 0.8 copy.19
  (14 shorter events, 0.2 us)
Async XLA Ops:
  33.5 23.0 %all-to-all-start.1 = ((bf16[4,8,200,128]{3,2,1,0:T(8,128)(2,1)}), bf16[4,8,200,128]{3,2,1,0:T(8,128)(2,1)S(1)}, u32[]{:S(2)}, u32[]{:S(2)}) async-start(bf16[4,8,200,128]{3,2,1,0:T(8,128)(2,1)} %broadcast_in_dim.75), calls=%async_computation.1 | async-start | bytes 3276800 | tf_op jit(solution)/shard_map/all_to_all | solution.py:163
  56.6 1.4 %copy-start = (bf16[4,8,200,128]{3,2,1,0:T(8,128)(2,1)}, bf16[4,8,200,128]{3,2,1,0:T(8,128)(2,1)S(1)}, u32[]{:S(2)}) copy-start(bf16[4,8,200,128]{3,2,1,0:T(8,128)(2,1)S(1)} %all-to-all-done.1) | copy-start | bytes 4915204
  93.6 17.4 %all-to-all-start.3 = ((bf16[16,24,512]{2,1,0:T(8,128)(2,1)}), bf16[16,24,512]{2,1,0:T(8,128)(2,1)S(1)}, u32[]{:S(2)}, u32[]{:S(2)}) async-start(bf16[16,24,512]{2,1,0:T(8,128)(2,1)} %broadcast_in_dim.76), calls=%async_computation.3 | async-start | bytes 786432 | tf_op jit(solution)/shard_map/all_to_all | solution.py:163

commit v4 on v3

v4 whole, which is shorter than its diff:
```python
import math

import jax
import jax.numpy as jnp
import numpy as np
from jax import lax
from jax.experimental import pallas as pl
from jax.experimental.pallas import tpu as pltpu
from jax.sharding import Mesh
from jax.sharding import PartitionSpec as P

KEPT = 448
PERIOD = 2 * KEPT
BINS, SLOTS, SITES, STEPS, ROWS = 14, 40, 21, 420, 16
SOURCES = KEPT // BINS
CHUNKS, HALVES = 6, 5
DEPTH = HALVES * SLOTS
TALL = SOURCES * CHUNKS * 8
WIDE = 512
X, Z, Y, C = "freq_0", "freq_1", "sens_0", "sens_1"
FREQ = (X, Z)
SENS = (Y, C)
f32, bf16 = jnp.float32, jnp.bfloat16
PLAIN = (((1,), (0,)), ((), ()))
TURNED = (((1,), (1,)), ((), ()))


def base_table():
    k = np.arange(KEPT)[:, None]
    t = np.arange(STEPS)[None, :]
    a = ((k * t) % PERIOD) * (2.0 * np.pi / PERIOD)
    return np.stack([np.cos(a), -np.sin(a)], axis=1)


def chunk_rows():
    table = base_table().reshape(SOURCES, BINS, 2, STEPS)
    table = np.pad(table, ((0, 0), (0, 2), (0, 0), (0, WIDE - STEPS)))
    parts = [table[:, 5 * g // 2 : 5 * g // 2 + 4] for g in range(CHUNKS)]
    return np.stack(parts, axis=1).swapaxes(2, 3).reshape(TALL, WIDE)


def chunk_masks():
    same = np.zeros((CHUNKS, 2, 4, 256), np.float32)
    swap = np.zeros((CHUNKS, 2, 4, 256), np.float32)
    for g in range(CHUNKS):
        for h in range(HALVES):
            half = 5 * g + h
            if half < 2 * BINS:
                b = half // 2 - 5 * g // 2
                lanes = slice(h * SLOTS, (h + 1) * SLOTS)
                if half % 2 == 0:
                    same[g, :, b, lanes] = 1.0
                else:
                    swap[g, 0, b, lanes] = -1.0
                    swap[g, 1, b, lanes] = 1.0
    return same.reshape(CHUNKS, 8, 256), swap.reshape(CHUNKS, 8, 256)


def spread_kernel(x_ref, live_ref, table_ref, same_ref, swap_ref, out_ref, inv_ref, x5_ref):
    @pl.when(pl.program_id(0) == 0)
    def _():
        rows = table_ref[...].astype(f32)
        place = lax.broadcasted_iota(jnp.int32, (TALL, WIDE), 0)
        inv_ref[...] = (rows * jnp.where((place == 0) | (place == 4), 0.5, 1.0)).T.astype(bf16)
        x5_ref[...] = jnp.zeros_like(x5_ref)

    halves = []
    for j in range(2):
        x = x_ref[j] * live_ref[...]
        for h in range(HALVES):
            x5_ref[j, h * SLOTS : (h + 1) * SLOTS, :STEPS] = x
        d = lax.dot_general(table_ref[...], x5_ref[j], TURNED, preferred_element_type=f32)
        d = d.reshape(SOURCES, CHUNKS, 8, 256)
        halves.append(d * same_ref[...][None] + pltpu.roll(d, 4, 2) * swap_ref[...][None])
    out_ref[...] = jnp.concatenate(halves, axis=2).astype(bf16)


def spread(samples, live):
    same, swap = chunk_masks()
    return pl.pallas_call(
        spread_kernel,
        grid=(ROWS // 2,),
        in_specs=[
            pl.BlockSpec((2, SLOTS, STEPS), lambda p: (p, 0, 0)),
            pl.BlockSpec((SLOTS, 1), lambda p: (0, 0)),
            pl.BlockSpec((TALL, WIDE), lambda p: (0, 0)),
            pl.BlockSpec((CHUNKS, 8, 256), lambda p: (0, 0, 0)),
            pl.BlockSpec((CHUNKS, 8, 256), lambda p: (0, 0, 0)),
        ],
        out_specs=[
            pl.BlockSpec((SOURCES, CHUNKS, 16, 256), lambda p: (0, 0, p, 0)),
            pl.BlockSpec((WIDE, TALL), lambda p: (0, 0)),
        ],
        out_shape=[
            jax.ShapeDtypeStruct((SOURCES, CHUNKS, 8 * ROWS, 256), bf16),
            jax.ShapeDtypeStruct((WIDE, TALL), bf16),
        ],
        scratch_shapes=[pltpu.VMEM((2, 256, WIDE), bf16)],
        cost_estimate=pl.CostEstimate(
            flops=2 * TALL * WIDE * 256 * ROWS, transcendentals=0, bytes_accessed=16_000_000
        ),
        name="spread",
    )(samples, live, jnp.asarray(chunk_rows(), bf16), jnp.asarray(same), jnp.asarray(swap))


def three(v):
    hi = v.astype(bf16).astype(f32)
    mid = (v - hi).astype(bf16).astype(f32)
    return hi, mid, v - hi - mid


BLOCK, SLOTS_AHEAD = 2, 4


def finish_kernel(left_ref, gath_ref, inv_ref, noise_ref, out_ref, z_ref, held, inv_held, sems, inv_sem):
    count = SOURCES // BLOCK
    lane = lax.broadcasted_iota(jnp.int32, (4, 8, 128), 2)

    def fetch(b):
        slot = lax.rem(b, SLOTS_AHEAD)
        return pltpu.make_async_copy(
            left_ref.at[pl.ds(b * BLOCK, BLOCK)], held.at[slot], sems.at[slot]
        )

    inverse = pltpu.make_async_copy(inv_ref, inv_held, inv_sem)
    for b in range(SLOTS_AHEAD - 1):
        fetch(b).start()
    inverse.start()
    first = gath_ref[0].astype(f32)
    where = lax.broadcasted_iota(jnp.int32, (DEPTH, 128), 0) < 2 * SLOTS
    where &= lax.broadcasted_iota(jnp.int32, (DEPTH, 128), 1) < SITES

    def some(b, squares):
        @pl.when(b + SLOTS_AHEAD - 1 < count)
        def _():
            fetch(b + SLOTS_AHEAD - 1).start()

        fetch(b).wait()
        slot = lax.rem(b, SLOTS_AHEAD)
        for i in range(BLOCK):
            f = b * BLOCK + i
            block = gath_ref[f]
            wide = block.astype(f32)
            squares = squares + wide * wide
            left = held[slot, i].reshape(CHUNKS * 8 * ROWS, 256)[:, :DEPTH]
            prod = lax.dot_general(left, block, PLAIN, preferred_element_type=f32)
            prod = prod.reshape(CHUNKS, 4, 4, 8, 128)
            packed = []
            for g in range(CHUNKS):
                acc = jnp.zeros((4, 8, 128), f32)
                for r in range(4):
                    moved = pltpu.roll(prod[g, :, r], (32 * r - SITES * g) % 128, 2)
                    acc = jnp.where((lane >= 32 * r) & (lane < 32 * r + SITES), moved, acc)
                packed.append(acc)
            start = pl.multiple_of(f * CHUNKS * 8, 16)
            for q in range(4):
                col = jnp.concatenate([packed[g][q] for g in range(CHUNKS)], axis=0)
                z_ref[pl.ds(start, CHUNKS * 8), 128 * q : 128 * (q + 1)] = col.astype(bf16)
        return squares

    squares = lax.fori_loop(0, count, some, jnp.where(where, -0.5 * first * first, 0.0))
    spots = jnp.sum(squares * noise_ref[...], axis=0, keepdims=True) * (2.0 / PERIOD)
    noise = spots
    for g in range(1, CHUNKS):
        noise = noise + pltpu.roll(spots, 128 - SITES * g, 1)
    noise = jnp.where(lax.broadcasted_iota(jnp.int32, (1, 128), 1) < SITES, noise, 0.0)
    noise = jnp.concatenate([noise, jnp.zeros((1, WIDE - 128), f32)], axis=1)
    row = lax.broadcasted_iota(jnp.int32, (32, WIDE), 0)
    tail = jnp.zeros((32, WIDE), f32)
    for n, part in enumerate(three(noise)):
        tail = jnp.where(row == SITES + n, part, tail)
    inverse.wait()
    total = lax.dot_general(inv_held[...], z_ref[...], PLAIN, preferred_element_type=f32)
    total = (total.T * (2.0 / PERIOD)).reshape(ROWS, 32, WIDE) + tail[None]
    out_ref[...] = total[:, :24].astype(bf16)


def finish(left, gathered, inverse, slot_noise):
    vmem = pl.BlockSpec(memory_space=pltpu.VMEM)
    hbm = pl.BlockSpec(memory_space=pl.ANY)
    return pl.pallas_call(
        finish_kernel,
        in_specs=[hbm, vmem, hbm, vmem],
        out_specs=vmem,
        out_shape=jax.ShapeDtypeStruct((ROWS, 24, WIDE), bf16),
        scratch_shapes=[
            pltpu.VMEM((TALL, 4 * 128), bf16),
            pltpu.VMEM((SLOTS_AHEAD, BLOCK, CHUNKS, 8 * ROWS, 256), bf16),
            pltpu.VMEM((WIDE, TALL), bf16),
            pltpu.SemaphoreType.DMA((SLOTS_AHEAD,)),
            pltpu.SemaphoreType.DMA,
        ],
        name="finish",
    )(left, gathered, inverse, slot_noise)


def total_kernel(got_ref, rep_ref, noise_ref):
    total = jnp.sum(got_ref[...].astype(f32), axis=0)
    rep_ref[...] = jnp.broadcast_to(total.astype(bf16)[None], rep_ref.shape)
    tail = total[16:24, :128]
    row = lax.broadcasted_iota(jnp.int32, tail.shape, 0)
    noise_ref[...] = jnp.sum(jnp.where(row >= SITES - 16, tail, 0.0), axis=0, keepdims=True)


def total_of(got):
    vmem = pl.BlockSpec(memory_space=pltpu.VMEM)
    return pl.pallas_call(
        total_kernel,
        in_specs=[vmem],
        out_specs=[vmem] * 2,
        out_shape=[
            jax.ShapeDtypeStruct(got.shape, bf16),
            jax.ShapeDtypeStruct((1, 128), f32),
        ],
        compiler_params=pltpu.CompilerParams(vmem_limit_bytes=8 << 20),
        name="total",
    )(got)


def share(array, axis):
    n = lax.axis_size(axis)
    return lax.all_to_all(
        jnp.broadcast_to(array[None], (n, *array.shape)), axis, 0, 0, tiled=True
    )


def payload_of(response, advance_offset, first_bin):
    k_own = first_bin + lax.iota(jnp.int32, BINS)
    turn = (k_own[:, None] * advance_offset[None, :]) % PERIOD
    ang = turn.astype(f32) * (2.0 * math.pi / PERIOD)
    cos, sin = jnp.cos(ang)[:, None, :], jnp.sin(ang)[:, None, :]
    re, im = response[:, 0].astype(f32), response[:, 1].astype(f32)
    turned = jnp.stack([re * cos - im * sin, re * sin + im * cos], axis=1).astype(bf16)
    half = turned.reshape(2 * BINS, SLOTS, SITES)
    half = jnp.pad(half, ((0, CHUNKS * HALVES - 2 * BINS), (0, 0), (0, 0)))
    half = half.reshape(CHUNKS, DEPTH, SITES).transpose(1, 0, 2).reshape(DEPTH, CHUNKS * SITES)
    return jnp.pad(half, ((0, 0), (0, 128 - CHUNKS * SITES)))


def noise_of(slot_sensor, sensor_noise):
    ids = lax.iota(jnp.int32, sensor_noise.shape[0])
    slot_noise = jnp.sum(
        jnp.where(slot_sensor[:, None] == ids[None, :], sensor_noise[None, :], 0.0), axis=1
    )
    return jnp.tile(slot_noise, HALVES)[:, None]


def on_device(samples, response, slot_sensor, sensor_noise, advance_offset):
    first_bin = lax.axis_index(FREQ) * BINS
    payload = payload_of(response, advance_offset, first_bin)
    gathered = share(share(payload, Z), X).reshape(SOURCES, DEPTH, 128)
    left, inverse = spread(samples, (slot_sensor >= 0).astype(bf16)[:, None])
    piece = finish(left, gathered, inverse, noise_of(slot_sensor, sensor_noise))
    got = lax.all_to_all(piece, SENS, 0, 0, tiled=True)
    copies, noise = total_of(got)
    outlook = lax.all_to_all(copies, SENS, 0, 0, tiled=True)[:, :SITES, :STEPS]
    return outlook, noise[0, :SITES]


def solution(mesh):
    torus = Mesh(mesh.devices.reshape(4, 8, 8, 2), (X, Z, Y, C))
    return jax.shard_map(
        on_device,
        mesh=torus,
        in_specs=(P(FREQ, SENS, None), P(FREQ, None, SENS, None), P(SENS), P(), P()),
        out_specs=(P(FREQ, None, None), P()),
        check_vma=False,
    )
```

time: 112 us -> 111 us (level)
  other arithmetic: 8.01 us -> 3.15 us
  waiting for transfers between devices: 13.4 us -> 17.3 us
  Pallas kernels: 28.8 us -> 25.9 us
  local copies, waits for them, and re-layouts: 4.08 us -> 6.21 us
    all_to_all x0 -> x1, waiting for transfers between devices: none -> 13.4 us  [on_device(): outlook = lax.all_to_all(copies, SENS, 0, 0, tiled=True)[:, :SITES, :STEPS]]
    all_to_all x2 -> x1, waiting for transfers between devices: 13.4 us -> 3.88 us  [share(): lax.all_to_all(jnp.broadcast_to(array[None], (n, *array.shape)), axis, 0,...]
    pallas_call x1, Pallas kernels: 19 us -> 13.4 us  [spread(): pl.pallas_call(spread_kernel, grid=(ROWS // 2,), in_specs=[pl.BlockSpec((...]
    all_to_all x0 -> x1, starting transfers between devices: none -> 3.45 us  [on_device(): outlook = lax.all_to_all(copies, SENS, 0, 0, tiled=True)[:, :SITES, :STEPS]]
    reduce_sum x6 -> x1, other arithmetic: 3.55 us -> 0.18 us  [noise_of(): jnp.sum(jnp.where(slot_sensor[:, None] == ids[None, :], sensor_noise[None...]
    all_to_all x2 -> x1, starting transfers between devices: 7.46 us -> 4.14 us  [share(): lax.all_to_all(jnp.broadcast_to(array[None], (n, *array.shape)), axis, 0,...]
    pallas_call x1 -> x2, Pallas kernels: 9.77 us -> 12.6 us  [the longest x1 11.8 us: finish(): pl.pallas_call(finish_kernel, in_specs=[hbm, vmem, hbm, vmem], out_specs=...]
    unnamed x3 -> x8, local copies, waits for them, and re-layouts: 0.84 us -> 2.16 us
  transfers between devices with their start and end apart: 2 -> 2, of which waited for: 1 -> 2; matrix products, arithmetic and copies ran while one was open for 0% -> 2% of each run, Pallas kernels for 17% -> 12%
where the time goes in v4:
time: 111 us; the launch traced here: 110 us
  blocking collectives  49.4 us (45%)
  Pallas kernels  25.9 us (23%)
  waiting for transfers between devices  17.3 us (16%)
  starting transfers between devices  7.59 us (7%)
  local copies, waits for them, and re-layouts  6.21 us (6%)
  other arithmetic  3.15 us (3%)
    all_to_all x1, blocking collectives, on_device(): got = lax.all_to_all(piece, SENS, 0, 0, tiled=True)  25 us
    all_to_all x1, blocking collectives, share(): lax.all_to_all(jnp.broadcast_to(array[None], (n, *array.shape)), axis, 0,...  24.3 us
    all_to_all x1, waiting for transfers between devices, on_device(): outlook = lax.all_to_all(copies, SENS, 0, 0, tiled=True)[:, :SITES, :STEPS]  13.4 us
    pallas_call x1, Pallas kernels, spread(): pl.pallas_call(spread_kernel, grid=(ROWS // 2,), in_specs=[pl.BlockSpec((...  13.4 us
    pallas_call x1, Pallas kernels, finish(): pl.pallas_call(finish_kernel, in_specs=[hbm, vmem, hbm, vmem], out_specs=...  11.8 us
    all_to_all x1, starting transfers between devices, share(): lax.all_to_all(jnp.broadcast_to(array[None], (n, *array.shape)), axis, 0,...  4.14 us
    all_to_all x1, waiting for transfers between devices, share(): lax.all_to_all(jnp.broadcast_to(array[None], (n, *array.shape)), axis, 0,...  3.88 us
    all_to_all x1, starting transfers between devices, on_device(): outlook = lax.all_to_all(copies, SENS, 0, 0, tiled=True)[:, :SITES, :STEPS]  3.45 us
  transfers between devices with their start and end apart: 2, of which 2 were waited for; matrix products, arithmetic and copies ran while one was open for 2% of the time, Pallas kernels for 12%

profile of v4, /device:TPU:1, one launch (start us, length us, event | category | flops | bytes accessed | tf_op | source)
XLA Modules:
  0.0 110.3 jit_solution(527872094572869097)
XLA Ops:
  0.6 0.8 fusion.5
  1.4 1.8 %subtract_convert_fusion = (bf16[14,1,40,21]{2,1,3,0:T(2,128)(2,1)S(1)}, bf16[14,1,40,21]{2,1,3,0:T(2,128)(2,1)S(1)}) fusion(bf16[14,2,40,21]{2,1,3,0:T(2,128)(2,1)} %param.9, f32[14,21]{1,0:T(8,128)S(1)} %get-tuple-element.19, f32[14,21]{1,0:T(8,128)S(1)} %get-tuple-element.18), kind=kLoop, calls=%fused_computation.2 | loop fusion | flops 117600 | bytes 96432 | tf_op jit(solution)/shard_map/convert.1
  3.2 0.4 pad_maximum_fusion
  3.6 0.1 copy.19
  3.7 0.2 convert_element_type.33
  4.0 0.2 reshape.78
  4.3 0.1 copy.24
  4.4 0.1 broadcast_in_dim.18
  4.5 24.3 %all_to_all.20 = bf16[8,200,128]{2,1,0:T(8,128)(2,1)S(1)} all-to-all(bf16[8,200,128]{2,1,0:T(8,128)(2,1)S(1)} %broadcast_in_dim.18), channel_id=1, replica_groups=mesh['freq_0'=4,'freq_1'=8,'sens_0'=8,'sens_1'=2] {'freq_1'}, dimensions={0} | all-to-all | bytes 819200 | tf_op jit(solution)/shard_map/all_to_all | solution.py:222
  28.8 1.4 %broadcast_in_dim.19 = bf16[4,8,200,128]{3,2,1,0:T(8,128)(2,1)} broadcast(bf16[8,200,128]{2,1,0:T(8,128)(2,1)S(1)} %all_to_all.20), dimensions={1,2,3} | broadcast | bytes 2048000 | tf_op jit(solution)/shard_map/broadcast_in_dim | solution.py:223
  30.2 0.0 copy-start.2
  30.2 0.0 copy-start.1
  30.2 4.1 %all-to-all-start.1 = ((bf16[4,8,200,128]{3,2,1,0:T(8,128)(2,1)}), bf16[4,8,200,128]{3,2,1,0:T(8,128)(2,1)S(1)}, u32[]{:S(2)}, u32[]{:S(2)}) async-start(bf16[4,8,200,128]{3,2,1,0:T(8,128)(2,1)} %broadcast_in_dim.19), calls=%async_computation.1 | async-start | bytes 3276800 | tf_op jit(solution)/shard_map/all_to_all | solution.py:222
  34.3 0.0 copy-done.2
  34.4 0.7 copy.18.live_ref
  35.1 0.0 copy-done.1
  35.1 0.2 select_reduce_fusion
  35.2 0.8 broadcast_in_dim_tile.4.noise_ref
  36.0 13.4 %spread.1 = (bf16[32,6,128,256]{3,2,1,0:T(8,128)(2,1)}, bf16[512,1536]{1,0:T(8,128)(2,1)}) custom-call(bf16[16,40,420]{2,1,0:T(8,128)(2,1)} %x_ref.1, bf16[40,1]{1,0:T(8,128)(2,1)} %copy.18.live_ref, bf16[1536,512]{1,0:T(8,128)(2,1)} %constant.41.clone.table_ref, f32[6,8,256]{2,1,0:T(8,128)} %constant.42.clone.same_ref, f32[6,8,256]{2,1,0:T(8,128)} %constant.43.clone.swap_ref), custom_call_target="tpu_custom_call" | custom-call | flops 6442450944 | bytes 16000000 | tf_op jit(solution)/shard_map/spread/pallas_call | solution.py:80
  49.4 3.9 %all-to-all-done.1 = bf16[4,8,200,128]{3,2,1,0:T(8,128)(2,1)S(1)} async-done(((bf16[4,8,200,128]{3,2,1,0:T(8,128)(2,1)}), bf16[4,8,200,128]{3,2,1,0:T(8,128)(2,1)S(1)}, u32[]{:S(2)}, u32[]{:S(2)}) %all-to-all-start.1) | async-done | bytes 1638432 | tf_op jit(solution)/shard_map/all_to_all | solution.py:222
  53.3 0.0 copy-start
  53.3 1.2 %copy-done = bf16[4,8,200,128]{3,2,1,0:T(8,128)(2,1)} copy-done((bf16[4,8,200,128]{3,2,1,0:T(8,128)(2,1)}, bf16[4,8,200,128]{3,2,1,0:T(8,128)(2,1)S(1)}, u32[]{:S(2)}) %copy-start) | copy-done | bytes 1638424
  54.5 11.8 %finish.1 = bf16[16,24,512]{2,1,0:T(8,128)(2,1)} custom-call(bf16[32,6,128,256]{3,2,1,0:T(8,128)(2,1)} %get-tuple-element.6.left_ref, bf16[32,200,128]{2,1,0:T(8,128)(2,1)} %bitcast.13, bf16[512,1536]{1,0:T(8,128)(2,1)} %get-tuple-element.7.inv_ref, f32[200,1]{1,0:T(8,128)} %broadcast_in_dim_tile.4.noise_ref), custom_call_target="tpu_custom_call" | custom-call | tf_op jit(solution)/shard_map/finish/pallas_call | solution.py:181
  66.2 25.0 %all_to_all.21.got_ref = bf16[16,24,512]{2,1,0:T(8,128)(2,1)S(1)} all-to-all(bf16[16,24,512]{2,1,0:T(8,128)(2,1)} %finish.1), channel_id=1, replica_groups=mesh['freq_0'=4,'freq_1'=8,'sens_0'=8,'sens_1'=2] {'sens_0','sens_1'}, dimensions={0} | all-to-all | bytes 786432 | tf_op jit(solution)/shard_map/all_to_all | solution.py:254
  91.3 0.8 total.1
  92.1 3.4 %all-to-all-start.3 = ((bf16[16,24,512]{2,1,0:T(8,128)(2,1)}), bf16[16,24,512]{2,1,0:T(8,128)(2,1)S(1)}, u32[]{:S(2)}, u32[]{:S(2)}) async-start(bf16[16,24,512]{2,1,0:T(8,128)(2,1)} %get-tuple-element.8), calls=%async_computation.3 | async-start | bytes 786432 | tf_op jit(solution)/shard_map/all_to_all | solution.py:256
  95.5 0.5 slice_bitcast_fusion
  96.0 13.4 %all-to-all-done.3 = bf16[16,24,512]{2,1,0:T(8,128)(2,1)S(1)} async-done(((bf16[16,24,512]{2,1,0:T(8,128)(2,1)}), bf16[16,24,512]{2,1,0:T(8,128)(2,1)S(1)}, u32[]{:S(2)}, u32[]{:S(2)}) %all-to-all-start.3) | async-done | bytes 393248 | tf_op jit(solution)/shard_map/all_to_all | solution.py:256
  109.4 0.8 copy.23
  (7 shorter events, 0.1 us)
Async XLA Ops:
  30.2 4.2 %copy-start.2 = (s32[40]{0:T(128)S(1)}, s32[40]{0:T(128)}, u32[]{:S(2)}) copy-start(s32[40]{0:T(128)} %param.10) | copy-start | bytes 484
  30.2 4.9 %copy-start.1 = (f32[600]{0:T(1024)S(1)}, f32[600]{0:T(1024)}, u32[]{:S(2)}) copy-start(f32[600]{0:T(1024)} %param.11) | copy-start | bytes 7204
  30.2 23.1 %all-to-all-start.1 = ((bf16[4,8,200,128]{3,2,1,0:T(8,128)(2,1)}), bf16[4,8,200,128]{3,2,1,0:T(8,128)(2,1)S(1)}, u32[]{:S(2)}, u32[]{:S(2)}) async-start(bf16[4,8,200,128]{3,2,1,0:T(8,128)(2,1)} %broadcast_in_dim.19), calls=%async_computation.1 | async-start | bytes 3276800 | tf_op jit(solution)/shard_map/all_to_all | solution.py:222
  53.3 1.2 %copy-start = (bf16[4,8,200,128]{3,2,1,0:T(8,128)(2,1)}, bf16[4,8,200,128]{3,2,1,0:T(8,128)(2,1)S(1)}, u32[]{:S(2)}) copy-start(bf16[4,8,200,128]{3,2,1,0:T(8,128)(2,1)S(1)} %all-to-all-done.1) | copy-start | bytes 4915204
  92.1 17.4 %all-to-all-start.3 = ((bf16[16,24,512]{2,1,0:T(8,128)(2,1)}), bf16[16,24,512]{2,1,0:T(8,128)(2,1)S(1)}, u32[]{:S(2)}, u32[]{:S(2)}) async-start(bf16[16,24,512]{2,1,0:T(8,128)(2,1)} %get-tuple-element.8), calls=%async_computation.3 | async-start | bytes 786432 | tf_op jit(solution)/shard_map/all_to_all | solution.py:256

commit v5 on v4

v5 whole, which is shorter than its diff:
```python
import math

import jax
import jax.numpy as jnp
import numpy as np
from jax import lax
from jax.experimental import pallas as pl
from jax.experimental.pallas import tpu as pltpu
from jax.sharding import Mesh
from jax.sharding import PartitionSpec as P

KEPT = 448
PERIOD = 2 * KEPT
BINS, SLOTS, SITES, STEPS, ROWS = 14, 40, 21, 420, 16
SOURCES = KEPT // BINS
CHUNKS, HALVES = 6, 5
DEPTH = HALVES * SLOTS
TALL = SOURCES * CHUNKS * 8
WIDE = 512
X, Z, Y, C = "freq_0", "freq_1", "sens_0", "sens_1"
FREQ = (X, Z)
SENS = (Y, C)
f32, bf16 = jnp.float32, jnp.bfloat16
PLAIN = (((1,), (0,)), ((), ()))
TURNED = (((1,), (1,)), ((), ()))


def base_table():
    k = np.arange(KEPT)[:, None]
    t = np.arange(STEPS)[None, :]
    a = ((k * t) % PERIOD) * (2.0 * np.pi / PERIOD)
    return np.stack([np.cos(a), -np.sin(a)], axis=1)


def chunk_rows():
    table = base_table().reshape(SOURCES, BINS, 2, STEPS)
    table = np.pad(table, ((0, 0), (0, 2), (0, 0), (0, WIDE - STEPS)))
    parts = [table[:, 5 * g // 2 : 5 * g // 2 + 4] for g in range(CHUNKS)]
    return np.stack(parts, axis=1).swapaxes(2, 3).reshape(TALL, WIDE)


def chunk_masks():
    same = np.zeros((CHUNKS, 2, 4, 256), np.float32)
    swap = np.zeros((CHUNKS, 2, 4, 256), np.float32)
    for g in range(CHUNKS):
        for h in range(HALVES):
            half = 5 * g + h
            if half < 2 * BINS:
                b = half // 2 - 5 * g // 2
                lanes = slice(h * SLOTS, (h + 1) * SLOTS)
                if half % 2 == 0:
                    same[g, :, b, lanes] = 1.0
                else:
                    swap[g, 0, b, lanes] = -1.0
                    swap[g, 1, b, lanes] = 1.0
    return same.reshape(CHUNKS, 8, 256), swap.reshape(CHUNKS, 8, 256)


def spread_kernel(
    pay_ref, x_ref, live_ref, noise_ref, table_ref, same_ref, swap_ref,
    rep_ref, out_ref, inv_ref, col_ref, x5_ref,
):
    rep_ref[...] = jnp.broadcast_to(pay_ref[...][None], rep_ref.shape)
    rows = table_ref[...].astype(f32)
    place = lax.broadcasted_iota(jnp.int32, (TALL, WIDE), 0)
    inv_ref[...] = (rows * jnp.where((place == 0) | (place == 4), 0.5, 1.0)).T.astype(bf16)
    x5_ref[...] = jnp.zeros_like(x5_ref)
    for h in range(HALVES):
        col_ref[h * SLOTS : (h + 1) * SLOTS] = noise_ref[...]

    def pair(p, carry):
        halves = []
        for j in range(2):
            x = x_ref[2 * p + j] * live_ref[...]
            for h in range(HALVES):
                x5_ref[j, h * SLOTS : (h + 1) * SLOTS, :STEPS] = x
            d = lax.dot_general(table_ref[...], x5_ref[j], TURNED, preferred_element_type=f32)
            d = d.reshape(SOURCES, CHUNKS, 8, 256)
            halves.append(d * same_ref[...][None] + pltpu.roll(d, 4, 2) * swap_ref[...][None])
        both = jnp.concatenate(halves, axis=2).astype(bf16)
        out_ref[:, :, pl.ds(pl.multiple_of(16 * p, 16), 16), :] = both
        return carry

    lax.fori_loop(0, ROWS // 2, pair, 0)


def spread(payload, samples, live, noise):
    same, swap = chunk_masks()
    vmem = pl.BlockSpec(memory_space=pltpu.VMEM)
    return pl.pallas_call(
        spread_kernel,
        in_specs=[vmem] * 7,
        out_specs=[vmem] * 4,
        out_shape=[
            pltpu.VMEM((8, DEPTH, 128), bf16),
            pltpu.VMEM((SOURCES, CHUNKS, 8 * ROWS, 256), bf16),
            pltpu.VMEM((WIDE, TALL), bf16),
            pltpu.VMEM((DEPTH, 1), f32),
        ],
        scratch_shapes=[pltpu.VMEM((2, 256, WIDE), bf16)],
        cost_estimate=pl.CostEstimate(
            flops=2 * TALL * WIDE * 256 * ROWS, transcendentals=0, bytes_accessed=16_000_000
        ),
        compiler_params=pltpu.CompilerParams(vmem_limit_bytes=24 << 20),
        name="spread",
    )(payload, samples, live, noise, jnp.asarray(chunk_rows(), bf16), jnp.asarray(same), jnp.asarray(swap))


def three(v):
    hi = v.astype(bf16).astype(f32)
    mid = (v - hi).astype(bf16).astype(f32)
    return hi, mid, v - hi - mid


UNROLL = 4


def finish_kernel(left_ref, gath_ref, inv_ref, noise_ref, out_ref, z_ref):
    lane = lax.broadcasted_iota(jnp.int32, (4, 8, 128), 2)
    first = gath_ref[0].astype(f32)
    where = lax.broadcasted_iota(jnp.int32, (DEPTH, 128), 0) < 2 * SLOTS
    where &= lax.broadcasted_iota(jnp.int32, (DEPTH, 128), 1) < SITES

    def some(s, squares):
        for i in range(UNROLL):
            f = s * UNROLL + i
            block = gath_ref[f]
            wide = block.astype(f32)
            squares = squares + wide * wide
            left = left_ref[f].reshape(CHUNKS * 8 * ROWS, 256)[:, :DEPTH]
            prod = lax.dot_general(left, block, PLAIN, preferred_element_type=f32)
            prod = prod.reshape(CHUNKS, 4, 4, 8, 128)
            packed = []
            for g in range(CHUNKS):
                acc = jnp.zeros((4, 8, 128), f32)
                for r in range(4):
                    moved = pltpu.roll(prod[g, :, r], (32 * r - SITES * g) % 128, 2)
                    acc = jnp.where((lane >= 32 * r) & (lane < 32 * r + SITES), moved, acc)
                packed.append(acc)
            start = pl.multiple_of(f * CHUNKS * 8, 16)
            for q in range(4):
                col = jnp.concatenate([packed[g][q] for g in range(CHUNKS)], axis=0)
                z_ref[pl.ds(start, CHUNKS * 8), 128 * q : 128 * (q + 1)] = col.astype(bf16)
        return squares

    squares = lax.fori_loop(
        0, SOURCES // UNROLL, some, jnp.where(where, -0.5 * first * first, 0.0)
    )
    spots = jnp.sum(squares * noise_ref[...], axis=0, keepdims=True) * (2.0 / PERIOD)
    noise = spots
    for g in range(1, CHUNKS):
        noise = noise + pltpu.roll(spots, 128 - SITES * g, 1)
    noise = jnp.where(lax.broadcasted_iota(jnp.int32, (1, 128), 1) < SITES, noise, 0.0)
    noise = jnp.concatenate([noise, jnp.zeros((1, WIDE - 128), f32)], axis=1)
    row = lax.broadcasted_iota(jnp.int32, (32, WIDE), 0)
    tail = jnp.zeros((32, WIDE), f32)
    for n, part in enumerate(three(noise)):
        tail = jnp.where(row == SITES + n, part, tail)
    total = lax.dot_general(inv_ref[...], z_ref[...], PLAIN, preferred_element_type=f32)
    total = (total.T * (2.0 / PERIOD)).reshape(ROWS, 32, WIDE) + tail[None]
    out_ref[...] = total[:, :24].astype(bf16)


def finish(left, gathered, inverse, slot_noise):
    vmem = pl.BlockSpec(memory_space=pltpu.VMEM)
    return pl.pallas_call(
        finish_kernel,
        in_specs=[vmem] * 4,
        out_specs=vmem,
        out_shape=pltpu.VMEM((ROWS, 24, WIDE), bf16),
        scratch_shapes=[pltpu.VMEM((TALL, 4 * 128), bf16)],
        compiler_params=pltpu.CompilerParams(vmem_limit_bytes=24 << 20),
        name="finish",
    )(left, gathered, inverse, slot_noise)


def total_kernel(got_ref, rep_ref, noise_ref):
    total = jnp.sum(got_ref[...].astype(f32), axis=0)
    rep_ref[...] = jnp.broadcast_to(total.astype(bf16)[None], rep_ref.shape)
    tail = total[16:24, :SITES]
    row = lax.broadcasted_iota(jnp.int32, tail.shape, 0)
    noise_ref[...] = jnp.sum(jnp.where(row >= SITES - 16, tail, 0.0), axis=0, keepdims=True)


def total_of(got):
    vmem = pl.BlockSpec(memory_space=pltpu.VMEM)
    return pl.pallas_call(
        total_kernel,
        in_specs=[vmem],
        out_specs=[vmem] * 2,
        out_shape=[
            pltpu.VMEM(got.shape, bf16),
            jax.ShapeDtypeStruct((1, SITES), f32),
        ],
        compiler_params=pltpu.CompilerParams(vmem_limit_bytes=8 << 20),
        name="total",
    )(got)


def share(array, axis):
    n = lax.axis_size(axis)
    return lax.all_to_all(
        jnp.broadcast_to(array[None], (n, *array.shape)), axis, 0, 0, tiled=True
    )


def payload_of(response, advance_offset, first_bin):
    k_own = first_bin + lax.iota(jnp.int32, BINS)
    turn = (k_own[:, None] * advance_offset[None, :]) % PERIOD
    ang = turn.astype(f32) * (2.0 * math.pi / PERIOD)
    cos, sin = jnp.cos(ang)[:, None, :], jnp.sin(ang)[:, None, :]
    re, im = response[:, 0].astype(f32), response[:, 1].astype(f32)
    turned = jnp.stack([re * cos - im * sin, re * sin + im * cos], axis=1).astype(bf16)
    half = turned.reshape(2 * BINS, SLOTS, SITES)
    half = jnp.pad(half, ((0, CHUNKS * HALVES - 2 * BINS), (0, 0), (0, 0)))
    half = half.reshape(CHUNKS, DEPTH, SITES).transpose(1, 0, 2).reshape(DEPTH, CHUNKS * SITES)
    return jnp.pad(half, ((0, 0), (0, 128 - CHUNKS * SITES)))


def noise_of(slot_sensor, sensor_noise):
    ids = lax.iota(jnp.int32, sensor_noise.shape[0])
    slot_noise = jnp.sum(
        jnp.where(slot_sensor[:, None] == ids[None, :], sensor_noise[None, :], 0.0), axis=1
    )
    return slot_noise[:, None]


def on_device(samples, response, slot_sensor, sensor_noise, advance_offset):
    first_bin = lax.axis_index(FREQ) * BINS
    payload = payload_of(response, advance_offset, first_bin)
    live = (slot_sensor >= 0).astype(bf16)[:, None]
    copies, left, inverse, column = spread(
        payload, samples, live, noise_of(slot_sensor, sensor_noise)
    )
    gathered = share(lax.all_to_all(copies, Z, 0, 0, tiled=True), X)
    gathered = gathered.reshape(SOURCES, DEPTH, 128)
    piece = finish(left, gathered, inverse, column)
    got = lax.all_to_all(piece, SENS, 0, 0, tiled=True)
    copies, noise = total_of(got)
    copies, noise = lax.optimization_barrier((copies, noise.reshape(SITES)))
    outlook = lax.all_to_all(copies, SENS, 0, 0, tiled=True)[:, :SITES, :STEPS]
    return outlook, noise


def solution(mesh):
    torus = Mesh(mesh.devices.reshape(4, 8, 8, 2), (X, Z, Y, C))
    return jax.shard_map(
        on_device,
        mesh=torus,
        in_specs=(P(FREQ, SENS, None), P(FREQ, None, SENS, None), P(SENS), P(), P()),
        out_specs=(P(FREQ, None, None), P()),
        check_vma=False,
    )
```

time: 111 us -> 114 us (1.027)
  blocking collectives: 49.4 us -> 89.1 us
  waiting for transfers between devices: 17.3 us -> 0 us
  Pallas kernels: 25.9 us -> 16.9 us
  starting transfers between devices: 7.59 us -> 0 us
  local copies, waits for them, and re-layouts: 6.21 us -> 2 us
  other arithmetic: 3.15 us -> 4.66 us
    all_to_all x0 -> x2, blocking collectives: none -> 41.5 us  [the longest x1 24.3 us: on_device(): gathered = share(lax.all_to_all(copies, Z, 0, 0, tiled=True), X)]
    all_to_all x2 -> x0, waiting for transfers between devices: 17.3 us -> none  [the longest x1 13.4 us: on_device(): outlook = lax.all_to_all(copies, SENS, 0, 0, tiled=True)[:, :SITES, :STEPS]]
    pallas_call x2, Pallas kernels: 25.1 us -> 16.4 us  [the longest x1 10 us: spread(): pl.pallas_call(spread_kernel, in_specs=[vmem] * 7, out_specs=[vmem] * 4,...]
    all_to_all x2 -> x0, starting transfers between devices: 7.59 us -> none  [the longest x1 4.14 us: share(): lax.all_to_all(jnp.broadcast_to(array[None], (n, *array.shape)), axis, 0,...]
    all_to_all x1, blocking collectives: 24.3 us -> 22.5 us  [share(): lax.all_to_all(jnp.broadcast_to(array[None], (n, *array.shape)), axis, 0,...]
    unnamed x8 -> x9, local copies, waits for them, and re-layouts: 2.16 us -> 0.86 us
    broadcast_in_dim x2 -> x1, local copies, waits for them, and re-layouts: 1.46 us -> 0.21 us  [share(): jnp.broadcast_to(array[None], (n, *array.shape))]
  transfers between devices with their start and end apart: 2 -> 0, of which waited for: 2 -> 0; matrix products, arithmetic and copies ran while one was open for 2% -> 0% of each run, Pallas kernels for 12% -> 0%
where the time goes in v5:
time: 114 us; the launch traced here: 113 us
  blocking collectives  89.1 us (78%)
  Pallas kernels  16.9 us (15%)
  other arithmetic  4.66 us (4%)
  local copies, waits for them, and re-layouts  2 us (2%)
    all_to_all x1, blocking collectives, on_device(): got = lax.all_to_all(piece, SENS, 0, 0, tiled=True)  25.1 us
    all_to_all x1, blocking collectives, on_device(): gathered = share(lax.all_to_all(copies, Z, 0, 0, tiled=True), X)  24.3 us
    all_to_all x1, blocking collectives, share(): lax.all_to_all(jnp.broadcast_to(array[None], (n, *array.shape)), axis, 0,...  22.5 us
    all_to_all x1, blocking collectives, on_device(): outlook = lax.all_to_all(copies, SENS, 0, 0, tiled=True)[:, :SITES, :STEPS]  17.2 us
    pallas_call x1, Pallas kernels, spread(): pl.pallas_call(spread_kernel, in_specs=[vmem] * 7, out_specs=[vmem] * 4,...  10 us
    pallas_call x1, Pallas kernels, finish(): pl.pallas_call(finish_kernel, in_specs=[vmem] * 4, out_specs=vmem, out_sh...  6.38 us

profile of v5, /device:TPU:1, one launch (start us, length us, event | category | flops | bytes accessed | tf_op | source)
XLA Modules:
  0.0 113.4 jit_solution(3171612719466175590)
XLA Ops:
  0.6 0.0 copy-start.2
  0.6 0.0 copy-start.3
  0.7 0.0 copy-start.1
  0.7 0.0 copy-start
  0.7 0.8 fusion.7
  1.5 0.9 select_reduce_fusion
  2.4 0.1 copy.22.live_ref
  2.5 0.1 copy.23.noise_ref
  2.6 0.8 fusion.5
  3.4 1.8 %subtract_convert_fusion = (bf16[14,1,40,21]{2,1,3,0:T(2,128)(2,1)S(1)}, bf16[14,1,40,21]{2,1,3,0:T(2,128)(2,1)S(1)}) fusion(bf16[14,2,40,21]{2,1,3,0:T(2,128)(2,1)} %param.9, f32[14,21]{1,0:T(8,128)S(1)} %get-tuple-element.27, f32[14,21]{1,0:T(8,128)S(1)} %get-tuple-element.26), kind=kLoop, calls=%fused_computation.2 | loop fusion | flops 117600 | bytes 96432 | tf_op jit(solution)/shard_map/convert.1
  5.1 0.4 pad_maximum_fusion
  5.6 0.1 copy.19
  5.7 0.2 convert_element_type.33
  6.0 0.2 reshape.79
  6.2 0.1 copy.21
  6.3 0.0 copy-done.2
  6.3 0.0 copy-done.3
  6.4 0.0 copy-done.1
  6.4 0.0 copy-done
  6.4 10.0 %spread.1 = (bf16[8,200,128]{2,1,0:T(8,128)(2,1)S(1)}, bf16[32,6,128,256]{3,2,1,0:T(8,128)(2,1)S(1)}, bf16[512,1536]{1,0:T(8,128)(2,1)S(1)}, f32[200,1]{1,0:T(8,128)S(1)}) custom-call(bf16[200,128]{1,0:T(8,128)(2,1)S(1)} %pad.9.pay_ref, bf16[16,40,420]{2,1,0:T(8,128)(2,1)S(1)} %copy-done, bf16[40,1]{1,0:T(8,128)(2,1)S(1)} %copy.22.live_ref, ...), custom_call_target="tpu_custom_call" | custom-call | flops 6442450944 | bytes 16000000 | tf_op jit(solution)/shard_map/spread/pallas_call | solution.py:90
  16.4 24.3 %all_to_all.20 = bf16[8,200,128]{2,1,0:T(8,128)(2,1)S(1)} all-to-all(bf16[8,200,128]{2,1,0:T(8,128)(2,1)S(1)} %get-tuple-element.11), channel_id=1, replica_groups=mesh['freq_0'=4,'freq_1'=8,'sens_0'=8,'sens_1'=2] {'freq_1'}, dimensions={0} | all-to-all | bytes 819200 | tf_op jit(solution)/shard_map/all_to_all | solution.py:235
  40.7 0.2 broadcast_in_dim.38
  41.0 22.5 %all_to_all.21 = bf16[4,8,200,128]{3,2,1,0:T(8,128)(2,1)S(1)} all-to-all(bf16[4,8,200,128]{3,2,1,0:T(8,128)(2,1)S(1)} %broadcast_in_dim.38), channel_id=1, replica_groups=mesh['freq_0'=4,'freq_1'=8,'sens_0'=8,'sens_1'=2] {'freq_0'}, dimensions={0} | all-to-all | bytes 3276800 | tf_op jit(solution)/shard_map/all_to_all | solution.py:202
  63.5 6.4 %finish.1 = bf16[16,24,512]{2,1,0:T(8,128)(2,1)S(1)} custom-call(bf16[32,6,128,256]{3,2,1,0:T(8,128)(2,1)S(1)} %get-tuple-element.10.left_ref, bf16[32,200,128]{2,1,0:T(8,128)(2,1)S(1)} %bitcast.13, bf16[512,1536]{1,0:T(8,128)(2,1)S(1)} %get-tuple-element.12.inv_ref, f32[200,1]{1,0:T(8,128)S(1)} %get-tuple-element.13.noise_ref), custom_call_target="tpu_custom_call" | custom-call | tf_op jit(solution)/shard_map/finish/pallas_call | solution.py:166
  69.8 25.1 %all_to_all.22.got_ref = bf16[16,24,512]{2,1,0:T(8,128)(2,1)S(1)} all-to-all(bf16[16,24,512]{2,1,0:T(8,128)(2,1)S(1)} %finish.1), channel_id=1, replica_groups=mesh['freq_0'=4,'freq_1'=8,'sens_0'=8,'sens_1'=2] {'sens_0','sens_1'}, dimensions={0} | all-to-all | bytes 786432 | tf_op jit(solution)/shard_map/all_to_all | solution.py:238
  94.9 0.5 total.1
  95.4 17.2 %all_to_all.23 = bf16[16,24,512]{2,1,0:T(8,128)(2,1)S(1)} all-to-all(bf16[16,24,512]{2,1,0:T(8,128)(2,1)S(1)} %get-tuple-element.16), channel_id=1, replica_groups=mesh['freq_0'=4,'freq_1'=8,'sens_0'=8,'sens_1'=2] {'sens_0','sens_1'}, dimensions={0} | all-to-all | bytes 786432 | tf_op jit(solution)/shard_map/all_to_all | solution.py:241
  112.6 0.8 copy.24
  (5 shorter events, 0.1 us)
Async XLA Ops:
  0.6 5.7 %copy-start.2 = (f32[6,8,256]{2,1,0:T(8,128)S(1)}, f32[6,8,256]{2,1,0:T(8,128)}, u32[]{:S(2)}) copy-start(f32[6,8,256]{2,1,0:T(8,128)} %constant.43.clone.swap_ref) | copy-start | bytes 147460
  0.6 5.7 %copy-start.3 = (f32[6,8,256]{2,1,0:T(8,128)S(1)}, f32[6,8,256]{2,1,0:T(8,128)}, u32[]{:S(2)}) copy-start(f32[6,8,256]{2,1,0:T(8,128)} %constant.42.clone.same_ref) | copy-start | bytes 147460
  0.7 5.7 %copy-start.1 = (bf16[1536,512]{1,0:T(8,128)(2,1)S(1)}, bf16[1536,512]{1,0:T(8,128)(2,1)}, u32[]{:S(2)}) copy-start(bf16[1536,512]{1,0:T(8,128)(2,1)} %constant.41.clone.table_ref) | copy-start | bytes 4718596
  0.7 5.7 %copy-start = (bf16[16,40,420]{2,1,0:T(8,128)(2,1)S(1)}, bf16[16,40,420]{2,1,0:T(8,128)(2,1)}, u32[]{:S(2)}) copy-start(bf16[16,40,420]{2,1,0:T(8,128)(2,1)} %x_ref.1) | copy-start | bytes 1612804
